TPU v7x, 32 devices: a whole 2x2x4 slice. The times are simulated.
32 devices in a mesh: seq: 16 (over z, x, core), head: 1, batch: 2 (over y).
Axes of the slice: x: 2, y: 2, z: 4, core: 2. Of those that a mesh axis runs over, the one named last changes fastest.
Arguments:
- queries: bfloat16 [2, 8192, 8, 8, 128], P('batch', 'seq', 'head'), may hold values from -160 to 160
- key_rows: bfloat16 [2, 8192, 8, 128], P('batch', 'seq'), may hold values from -6 to 6
- value_rows: bfloat16 [2, 8192, 8, 128], P('batch', 'seq'), may hold values from -6 to 6
- compressed: bfloat16 [2, 128, 8, 128], P('batch', 'seq'), may hold values from -6 to 6
- chosen: int32 [2, 128, 8, 16], P('batch', 'seq'), may hold values from 0 to 127, as said below
Outputs:
- block_scores: float32 [2, 128, 8, 128], P('batch', 'seq', 'head')
- attended: bfloat16 [2, 8192, 8, 8, 128], P('batch', 'seq', 'head')
Inputs may be any that keep to these rules, and one draw needn't show every extreme that they name: `chosen`: every entry is at most its own tile number, and entry 0 of every row is the tile's own block. Over the tiles of one device of seq and one group, at most 2 different blocks of any other device are named, and every device after the first names exactly 2 blocks of the first device for each group.
All inputs are finite; a program needn't handle non-finite values.
Results may differ from a plain program's by a relative error of at most 0.008.
Values may be sent and summed in bfloat16 or wider, within the bound.
A program may use at most 128 MiB of HBM per device.

v0:
```python
import functools
import math

import jax
import jax.numpy as jnp
from jax import lax
from jax.experimental import pallas as pl
from jax.experimental.pallas import tpu as pltpu
from jax.sharding import PartitionSpec as P

HPG = 8
BLOCK = 64
TOPN = 16
CAP = 2


def softmax_parts(scores):
    row_top = jnp.max(scores, axis=-1, keepdims=True)
    weights = jnp.exp(scores - row_top)
    return (weights, jnp.sum(weights, axis=-1, keepdims=True))


def attend_tile(shape, slot_ref, pick_ref, first_ref, query_ref, own_ref, remote_ref, out_ref, pool, picked):
    heads_local, blk_dev, shards, cap, block_len, head_width = shape
    group, tile = pl.program_id(0), pl.program_id(1)

    @pl.when(tile == 0)
    def _():
        pool[:blk_dev] = own_ref[0]
        for shard in range(shards):
            pool[blk_dev + shard * cap : blk_dev + (shard + 1) * cap] = remote_ref[shard, 0]

    tile_number = first_ref[0] + tile
    keys = TOPN * block_len
    column = lax.broadcasted_iota(jnp.int32, (1, keys), 1)
    within = column % block_len
    block_place = column // block_len
    limit = jnp.full((1, keys), -1, jnp.int32)
    for place in range(TOPN):
        picked[place * block_len : (place + 1) * block_len] = pool[slot_ref[tile, group, place]]
        is_own = pick_ref[tile, group, place] == tile_number
        limit = jnp.where((block_place == place) & is_own, within, limit)
    rows = block_len * heads_local
    part = min(rows, 256)
    factor = math.log2(math.e) * head_width ** (-0.5)
    for start in range(0, rows, part):
        query = query_ref[0, 0, start : start + part]
        scores = lax.dot_general(
            query,
            picked[:, :head_width],
            (((1,), (1,)), ((), ())),
            preferred_element_type=jnp.float32,
        )
        token = (start + lax.broadcasted_iota(jnp.int32, (part, 1), 0)) // heads_local
        scores = jnp.where(limit <= token, scores, -jnp.inf)
        row_top = jnp.max(scores, axis=-1, keepdims=True)
        weights = jnp.exp2((scores - row_top) * factor)
        totals = jnp.sum(weights, axis=-1, keepdims=True)
        mixed = jnp.dot(
            weights.astype(jnp.bfloat16),
            picked[:, head_width:],
            preferred_element_type=jnp.float32,
        )
        out_ref[0, 0, start : start + part] = (mixed / totals).astype(jnp.bfloat16)


def local(queries, key_rows, value_rows, compressed, chosen):
    _, tok_rows, heads_local, groups, head_width = queries.shape
    block_len = BLOCK
    shards = lax.axis_size("seq")
    seq_rank = lax.axis_index("seq")
    blk_dev = tok_rows // block_len
    nblk = blk_dev * shards
    score_scale = head_width ** (-0.5)
    query_rows = queries[0]
    query_pos = seq_rank * tok_rows + jnp.arange(tok_rows, dtype=jnp.int32)
    gathered = lax.all_gather(compressed, "seq", axis=1, tiled=True)
    logits = (
        jnp.einsum(
            "tjgd,ngd->tjgn",
            query_rows,
            gathered[0],
            preferred_element_type=jnp.float32,
        )
        * score_scale
    )
    all_blocks = jnp.arange(nblk, dtype=jnp.int32)
    seen = all_blocks[None, :] <= (query_pos // block_len)[:, None]
    logits = jnp.where(seen[:, None, None, :], logits, -jnp.inf)
    weights, totals = softmax_parts(logits)
    probability = weights / totals
    pooled = jnp.sum(
        probability.reshape(blk_dev, block_len, heads_local, groups, nblk), axis=(1, 2)
    )[None]
    shared = lax.psum_scatter(
        pooled.astype(jnp.bfloat16), "head", scatter_dimension=2, tiled=True
    ).astype(jnp.float32)
    tile_ids = seq_rank * blk_dev + jnp.arange(blk_dev, dtype=jnp.int32)
    factor = (tile_ids + 1).astype(jnp.float32) / (block_len * HPG)
    block_scores = shared * factor[None, :, None, None]
    pick_rows = chosen[0]
    onehot = pick_rows[..., None] == all_blocks
    needed = jnp.any(onehot, axis=(0, 2))
    owner_of = all_blocks // blk_dev
    needed = needed & (owner_of != seq_rank)[None, :]
    needed_grid = needed.reshape(groups, shards, blk_dev).astype(jnp.int32)
    rank_in = jnp.cumsum(needed_grid, axis=2) - needed_grid
    places = jnp.arange(CAP, dtype=jnp.int32)
    within = jnp.arange(blk_dev, dtype=jnp.int32)
    matched = (needed_grid[..., None] == 1) & (rank_in[..., None] == places)
    wanted = jnp.sum(jnp.where(matched, within[:, None], 0), axis=2)
    slot_of = blk_dev + owner_of[None, :] * CAP + rank_in.reshape(groups, nblk)
    slot_of = jnp.where(
        owner_of[None, :] == seq_rank, all_blocks[None, :] - seq_rank * blk_dev, slot_of
    )
    pool_index = jnp.sum(jnp.where(onehot, slot_of[None, :, None, :], 0), axis=3)
    key_local = key_rows[0].reshape(blk_dev, block_len, groups, head_width)
    value_local = value_rows[0].reshape(blk_dev, block_len, groups, head_width)
    own_rows = jnp.transpose(jnp.concatenate([key_local, value_local], axis=-1), (2, 0, 1, 3))
    requested = lax.all_to_all(
        jnp.transpose(wanted, (1, 0, 2)), "seq", split_axis=0, concat_axis=0, tiled=True
    )
    group_ids = jnp.arange(groups, dtype=jnp.int32)[None, :, None]
    found = jnp.take(
        own_rows.reshape(groups * blk_dev, block_len, 2 * head_width),
        group_ids * blk_dev + requested,
        axis=0,
        mode="clip",
    )
    found, _ = lax.optimization_barrier((found, gathered))
    fetched = lax.all_to_all(found, "seq", split_axis=0, concat_axis=0, tiled=True)
    rows = block_len * heads_local
    query_tiles = jnp.transpose(
        query_rows.reshape(blk_dev, rows, groups, head_width), (2, 0, 1, 3)
    )
    shape = (heads_local, blk_dev, shards, CAP, block_len, head_width)
    tile_spec = pl.BlockSpec((1, 1, rows, head_width), lambda g, t, *_: (g, t, 0, 0))
    attended = pl.pallas_call(
        functools.partial(attend_tile, shape),
        grid_spec=pltpu.PrefetchScalarGridSpec(
            num_scalar_prefetch=3,
            grid=(groups, blk_dev),
            in_specs=[
                tile_spec,
                pl.BlockSpec(
                    (1, blk_dev, block_len, 2 * head_width), lambda g, t, *_: (g, 0, 0, 0)
                ),
                pl.BlockSpec(
                    (shards, 1, CAP, block_len, 2 * head_width),
                    lambda g, t, *_: (0, g, 0, 0, 0),
                ),
            ],
            out_specs=tile_spec,
            scratch_shapes=[
                pltpu.VMEM((blk_dev + shards * CAP, block_len, 2 * head_width), jnp.bfloat16),
                pltpu.VMEM((TOPN * block_len, 2 * head_width), jnp.bfloat16),
            ],
        ),
        out_shape=jax.ShapeDtypeStruct((groups, blk_dev, rows, head_width), jnp.bfloat16),
        compiler_params=pltpu.CompilerParams(
            dimension_semantics=("arbitrary", "arbitrary"), vmem_limit_bytes=48 * 1024 * 1024
        ),
    )(pool_index, pick_rows, (seq_rank * blk_dev)[None], query_tiles, own_rows, fetched)
    attended = jnp.transpose(attended, (1, 2, 0, 3))
    attended = attended.reshape(1, tok_rows, heads_local, groups, head_width)
    return (block_scores, attended)


def solution(mesh):
    placed = (
        P("batch", "seq", "head", None, None),
        P("batch", "seq", None, None),
        P("batch", "seq", None, None),
        P("batch", "seq", None, None),
        P("batch", "seq", None, None),
    )
    return jax.shard_map(
        local,
        mesh=mesh,
        in_specs=placed,
        out_specs=(P("batch", "seq", "head", None), P("batch", "seq", "head", None, None)),
        check_vma=False,
    )
```

profile of v0, /device:TPU:11, one launch (start us, length us, event | category | flops | bytes accessed | tf_op | source)
XLA Modules:
  0.0 335.8 jit_solution(2306429952923470894)
XLA Ops:
  0.6 1.0 fusion.8
  1.6 0.1 reduce_or.12
  1.8 1.3 reduce_window_sum.13
  3.1 0.1 copy.52
  3.2 0.1 copy.51
  3.3 0.7 copy.53
  4.0 6.5 %all-to-all-start = ((s32[16,8,2]{1,2,0:T(2,128)}), s32[16,8,2]{1,2,0:T(2,128)S(1)}, u32[]{:S(2)}, u32[]{:S(2)}) async-start(s32[16,8,2]{1,2,0:T(2,128)} %copy.53), calls=%async_computation | async-start | bytes 32768 | tf_op jit(solution)/shard_map/all_to_all | solution.py:120
  10.5 0.7 copy.45
  11.2 15.9 %all_gather.3 = bf16[1,128,8,128]{3,1,2,0:T(8,128)(2,1)S(1)} all-gather(bf16[1,8,8,128]{3,1,2,0:T(8,128)(2,1)S(1)} %copy.45), channel_id=1, replica_groups=mesh['seq'=16,'head'=1,'batch'=2] {'seq'}, dimensions={1}, use_global_device_ids=true | all-gather | bytes 278528 | tf_op jit(solution)/shard_map/all_gather | solution.py:77
  27.1 1.4 copy.50
  28.5 1.4 copy.49
  29.9 1.8 pad_maximum_fusion
  31.7 0.0 all-to-all-done
  31.7 0.1 copy.54
  31.7 0.1 broadcast_add_fusion
  31.8 0.1 copy.55
  31.9 0.1 reshape.215
  32.1 10.1 %gather_fusion = bf16[256,64,256]{2,1,0:T(8,128)(2,1)} fusion(bf16[64,64,256]{2,1,0:T(8,128)(2,1)} %bitcast.46, s32[1024]{0:T(1024)S(1)} %pad_clamp_fusion), kind=kCustom, calls=%fused_computation | custom fusion | bytes 16778240 | tf_op jit(solution)/shard_map/jit(_take)/gather | solution.py:124
  42.2 11.5 %all-to-all-start.1 = ((bf16[16,8,2,64,256]{4,3,2,1,0:T(8,128)(2,1)}), bf16[16,8,2,64,256]{4,3,2,1,0:T(8,128)(2,1)}, u32[]{:S(2)}, u32[]{:S(2)}) async-start(bf16[16,8,2,64,256]{4,3,2,1,0:T(8,128)(2,1)} %bitcast.48), calls=%async_computation.1 | async-start | bytes 16777216 | tf_op jit(solution)/shard_map/all_to_all | solution.py:131
  53.7 0.1 reduce_window_sum.14
  53.8 7.9 %copy.48 = bf16[1,512,8,8,128]{4,2,1,3,0:T(8,128)(2,1)} copy(bf16[1,512,8,8,128]{4,3,2,1,0:T(8,128)(2,1)} %param.5) | data formatting | bytes 16777216 | tf_op args[0]
  61.7 38.4 %fusion.3 = f32[8,128,512,8]{2,1,3,0:T(8,128)} fusion(bf16[512,8,8,128]{3,2,1,0:T(8,128)(2,1)} %bitcast.47, bf16[1,128,8,128]{3,1,2,0:T(8,128)(2,1)S(1)} %all_gather.3), kind=kOutput, calls=%fused_computation.7 | convolution fusion | flops 1073741824 | bytes 25427968 | tf_op jit(solution)/shard_map/tjgd,ngd->tjgn/dot_general | solution.py:79
  100.1 17.2 %fusion = f32[512,8,8,128]{0,3,1,2:T(8,128)} fusion(f32[8,128,512,8]{2,1,3,0:T(8,128)} %fusion.3, pred[512,128]{0,1:T(8,128)(4,1)S(1)} %iota_compare_fusion.1), kind=kOutput, calls=%fused_computation.1 | output fusion | flops 21037312 | bytes 33619968 | tf_op jit(solution)/shard_map/div | solution.py:91
  117.3 0.0 copy-start
  117.3 20.3 %divide_reduce_fusion = f32[512,8,128]{0,2,1:T(8,128)} fusion(f32[512,8,8,128]{0,3,1,2:T(8,128)} %fusion, f32[8,128,512,8]{2,1,3,0:T(8,128)} %fusion.3, pred[512,128]{0,1:T(8,128)(4,1)S(1)} %iota_compare_fusion.1), kind=kOutput, calls=%fused_computation.5 | output fusion | flops 28868736 | bytes 35717120 | tf_op jit(solution)/shard_map/sub | solution.py:19
  137.7 3.0 copy.47
  140.7 0.0 copy-done
  140.7 1.3 select_reduce_fusion.slot_ref
  142.0 1.7 bitcast_reduce_fusion
  143.7 0.7 convert_multiply_fusion
  144.4 91.4 %all-to-all-done.1.remote_ref = bf16[16,8,2,64,256]{4,3,2,1,0:T(8,128)(2,1)} async-done(((bf16[16,8,2,64,256]{4,3,2,1,0:T(8,128)(2,1)}), bf16[16,8,2,64,256]{4,3,2,1,0:T(8,128)(2,1)}, u32[]{:S(2)}, u32[]{:S(2)}) %all-to-all-start.1) | async-done | bytes 8388640 | tf_op jit(solution)/shard_map/all_to_all | solution.py:131
  235.7 83.3 %shard_map.68 = bf16[8,8,512,128]{3,2,1,0:T(8,128)(2,1)} custom-call(s32[8,8,16]{2,1,0:T(8,128)S(1)} %select_reduce_fusion.slot_ref, s32[8,8,16]{2,1,0:T(8,128)S(1)} %bitcast.45, s32[1]{0:T(128)} %bitcast.8.first_ref, bf16[8,8,512,128]{3,2,1,0:T(8,128)(2,1)} %bitcast.49, bf16[8,8,64,256]{3,2,1,0:T(8,128)(2,1)S(1)} %get-tuple-element.17.own_ref, ...), custom_call_target="tpu_custom_call" | custom-call | tf_op jit(solution)/shard_map/pallas_call | solution.py:138
  319.1 16.5 %copy.56 = bf16[1,512,8,8,128]{4,3,2,1,0:T(8,128)(2,1)} copy(bf16[1,512,8,8,128]{4,2,1,3,0:T(8,128)(2,1)} %bitcast.50) | data formatting | bytes 16777216
  (12 shorter events, 0.2 us)
Async XLA Ops:
  4.0 27.7 %all-to-all-start = ((s32[16,8,2]{1,2,0:T(2,128)}), s32[16,8,2]{1,2,0:T(2,128)S(1)}, u32[]{:S(2)}, u32[]{:S(2)}) async-start(s32[16,8,2]{1,2,0:T(2,128)} %copy.53), calls=%async_computation | async-start | bytes 32768 | tf_op jit(solution)/shard_map/all_to_all | solution.py:120
  42.2 193.5 %all-to-all-start.1 = ((bf16[16,8,2,64,256]{4,3,2,1,0:T(8,128)(2,1)}), bf16[16,8,2,64,256]{4,3,2,1,0:T(8,128)(2,1)}, u32[]{:S(2)}, u32[]{:S(2)}) async-start(bf16[16,8,2,64,256]{4,3,2,1,0:T(8,128)(2,1)} %bitcast.48), calls=%async_computation.1 | async-start | bytes 16777216 | tf_op jit(solution)/shard_map/all_to_all | solution.py:131
  117.3 23.3 %copy-start = (s32[1,8,8,16]{3,2,1,0:T(8,128)S(1)}, s32[1,8,8,16]{3,2,1,0:T(8,128)}, u32[]{:S(2)}) copy-start(s32[1,8,8,16]{3,2,1,0:T(8,128)} %param.9) | copy-start | bytes 12292
where the time goes:
time: 340 us; the launch traced here: 336 us
  waiting for transfers between devices  91.4 us (27%)
  Pallas kernels  83.3 us (24%)
  other arithmetic  45.6 us (13%)
  local copies, waits for them, and re-layouts  42.3 us (12%)
  matrix products  38.4 us (11%)
  starting transfers between devices  18 us (5%)
  blocking collectives  15.9 us (5%)
    all_to_all x1, waiting for transfers between devices, local(): lax.all_to_all(found, 'seq', split_axis=0, concat_axis=0, tiled=True)  91.4 us
    pallas_call x1, Pallas kernels, local(): pl.pallas_call(functools.partial(attend_tile, shape), grid_spec=pltpu.Pre...  83.3 us
    dot_general x1, matrix products, local(): jnp.einsum('tjgd,ngd->tjgn', query_rows, gathered[0], preferred_element_t...  38.4 us
    unnamed x7, local copies, waits for them, and re-layouts  27.8 us
    sub x1, other arithmetic, softmax_parts(): weights = jnp.exp(scores - row_top)  20.3 us
    div x1, other arithmetic, local(): probability = weights / totals  17.2 us
    all_gather x1, blocking collectives, local(): gathered = lax.all_gather(compressed, 'seq', axis=1, tiled=True)  15.9 us
    all_to_all x1, starting transfers between devices, local(): lax.all_to_all(found, 'seq', split_axis=0, concat_axis=0, tiled=True)  11.5 us
  transfers between devices with their start and end apart: 2, of which 1 were waited for; matrix products, arithmetic and copies ran while one was open for 29% of the time, Pallas kernels for 0%

commit v1 on v0

v1 whole, which is shorter than its diff:
```python
import functools
import math

import jax
import jax.numpy as jnp
from jax import lax
from jax.experimental import pallas as pl
from jax.experimental.pallas import tpu as pltpu
from jax.sharding import PartitionSpec as P

HPG = 8
BLOCK = 64
TOPN = 16
CAP = 2
COLS = 2
CORES = 2
MESH = pl.DeviceIdType.MESH


def mega(
    shape,
    slot_ref,
    pick_ref,
    wanted_ref,
    own_ref,
    query_ref,
    out_ref,
    pooled_ref,
    column,
    peer_out,
    peer_in,
    cur,
    comp,
    queries,
    mixed_out,
    picked,
    peer_wanted,
    peer_wanted_s,
    up_send,
    up_recv,
    sib_send,
    sib_recv,
    peer_send,
    peer_recv,
    own_sem,
    query_sem,
    out_sem,
    misc_sem,
):
    levels, groups, blk_dev, heads_local, block_len, head_width = shape
    rows = block_len * heads_local
    tokens = blk_dev * block_len
    per_level = COLS * CORES
    slots_col = levels * CORES * blk_dev
    picks = CORES * CAP

    rank = lax.axis_index("seq")
    core = lax.rem(rank, CORES)
    col = lax.rem(rank // CORES, COLS)
    level = rank // per_level
    sibling = rank + 1 - 2 * core
    peer = rank + CORES * (1 - 2 * col)
    above = rank + per_level
    below = rank - per_level
    has_above = level < levels - 1
    has_below = level > 0

    barrier = pltpu.get_barrier_semaphore()
    for other in (sibling, peer):
        pl.semaphore_signal(barrier, inc=1, device_id={"seq": other}, device_id_type=MESH)

    @pl.when(has_above)
    def _():
        pl.semaphore_signal(barrier, inc=1, device_id={"seq": above}, device_id_type=MESH)

    @pl.when(has_below)
    def _():
        pl.semaphore_signal(barrier, inc=1, device_id={"seq": below}, device_id_type=MESH)

    def own_copy(g):
        return pltpu.make_async_copy(own_ref.at[g], column.at[level, core, g], own_sem.at[g])

    def query_copy(g):
        return pltpu.make_async_copy(query_ref.at[g], queries.at[g], query_sem.at[g])

    def out_copy(g):
        return pltpu.make_async_copy(mixed_out.at[g], out_ref.at[g], out_sem.at[g])

    def up(l, g):
        part = column.at[l, core, g]
        return pltpu.make_async_remote_copy(
            part, part, up_send.at[l, g], up_recv.at[l, g], device_id={"seq": above}, device_id_type=MESH
        )

    def aside(l, g, owner):
        part = column.at[l, owner, g]
        return pltpu.make_async_remote_copy(
            part, part, sib_send.at[l, g], sib_recv.at[l, g], device_id={"seq": sibling}, device_id_type=MESH
        )

    def across(l, g):
        return pltpu.make_async_remote_copy(
            peer_out.at[g, l],
            peer_in.at[g, l],
            peer_send.at[l, g],
            peer_recv.at[l, g],
            device_id={"seq": peer},
            device_id_type=MESH,
        )

    wanted_copy = pltpu.make_async_remote_copy(
        wanted_ref, peer_wanted, misc_sem.at[0], misc_sem.at[1], device_id={"seq": peer}, device_id_type=MESH
    )

    def loop(n, body):
        def step(i, carry):
            body(i)
            return carry

        lax.fori_loop(0, n, step, 0)

    loop(groups, lambda g: own_copy(g).start())
    loop(groups, lambda g: query_copy(g).start())
    comp[...] = jnp.zeros_like(comp)

    count = 2 + has_above.astype(jnp.int32) + has_below.astype(jnp.int32)
    pl.semaphore_wait(barrier, count)
    wanted_copy.start()

    def pass_on(l, g):
        @pl.when(has_above)
        def _():
            up(l, g).start()

        aside(l, g, core).start()

    def forward(g):
        own_copy(g).wait()
        pass_on(level, g)

        def relay(i):
            l = level - 1 - i
            up(l, g).wait_recv()
            pass_on(l, g)

        loop(level, relay)

    def take_column(g):
        half = lax.rem(g, 2)

        def body(l):
            aside(l, g, 1 - core).wait_recv()
            for c in range(CORES):
                first = (l * CORES + c) * blk_dev
                for b in range(blk_dev):
                    cur[half, first + b] = column[l, c, g, b * block_len : (b + 1) * block_len]
                keys = column[l, c, g, tokens : tokens + blk_dev, :head_width]
                comp[half, (l * COLS + col) * CORES + c] = keys.astype(jnp.float32)

        loop(level + 1, body)

    def serve_peer(g):
        half = lax.rem(g, 2)

        def body(l):
            for c in range(CORES):
                source = (l * COLS + col) * CORES + c
                for k in range(CAP):
                    index = peer_wanted_s[g, source * CAP + k]
                    place = (c * CAP + k) * block_len
                    peer_out[g, l, place : place + block_len] = cur[half, (l * CORES + c) * blk_dev + index]
            first = (l * COLS + col) * CORES
            keys = comp[half, pl.ds(first, CORES)].reshape(CORES * blk_dev, head_width)
            keys = keys.astype(jnp.bfloat16)
            peer_out[g, l, picks * block_len :] = jnp.concatenate([keys, keys], axis=1)
            across(l, g).start()

        loop(level + 1, body)

    def take_peer(g):
        half = lax.rem(g, 2)

        def body(l):
            across(l, g).wait_recv()
            for k in range(picks):
                cur[half, slots_col + l * picks + k] = peer_in[g, l, k * block_len : (k + 1) * block_len]
            keys = peer_in[g, l, picks * block_len :, :head_width].astype(jnp.float32)
            first = (l * COLS + 1 - col) * CORES
            comp[half, pl.ds(first, CORES)] = keys.reshape(CORES, blk_dev, head_width)

        loop(level + 1, body)

    factor = math.log2(math.e) * head_width ** (-0.5)
    part = min(rows, 256)
    keys_all = TOPN * block_len
    nblk = levels * per_level * blk_dev

    def compute(g):
        half = lax.rem(g, 2)
        query_copy(g).wait()
        key_position = lax.broadcasted_iota(jnp.int32, (1, keys_all), 1)
        within = key_position % block_len
        block_place = key_position // block_len
        block_number = lax.broadcasted_iota(jnp.int32, (1, nblk), 1)

        def tile_body(t):
            tile_number = rank * blk_dev + t
            limit = jnp.full((1, keys_all), -1, jnp.int32)
            for place in range(TOPN):
                picked[place * block_len : (place + 1) * block_len] = cur[half, slot_ref[t, g, place]]
                is_own = pick_ref[t, g, place] == tile_number
                limit = jnp.where((block_place == place) & is_own, within, limit)
            summary = comp[half].reshape(nblk, head_width).astype(jnp.bfloat16)
            pooled = jnp.zeros((1, nblk), jnp.float32)
            for start in range(0, rows, part):
                query = queries[g, t, start : start + part]
                logits = lax.dot_general(
                    query, summary, (((1,), (1,)), ((), ())), preferred_element_type=jnp.float32
                )
                logits = jnp.where(block_number <= tile_number, logits, -jnp.inf)
                top = jnp.max(logits, axis=-1, keepdims=True)
                weights = jnp.exp2((logits - top) * factor)
                totals = jnp.sum(weights, axis=-1, keepdims=True)
                pooled += jnp.sum(weights / totals, axis=0, keepdims=True)

                scores = lax.dot_general(
                    query, picked[:, :head_width], (((1,), (1,)), ((), ())), preferred_element_type=jnp.float32
                )
                token = (start + lax.broadcasted_iota(jnp.int32, (part, 1), 0)) // heads_local
                scores = jnp.where(limit <= token, scores, -jnp.inf)
                row_top = jnp.max(scores, axis=-1, keepdims=True)
                weights = jnp.exp2((scores - row_top) * factor)
                totals = jnp.sum(weights, axis=-1, keepdims=True)
                mixed = jnp.dot(
                    weights.astype(jnp.bfloat16), picked[:, head_width:], preferred_element_type=jnp.float32
                )
                mixed_out[g, t, start : start + part] = (mixed / totals).astype(jnp.bfloat16)
            pooled_ref[pl.ds(t * groups + g, 1), :] = pooled

        loop(blk_dev, tile_body)
        out_copy(g).start()

    forward(0)
    wanted_copy.wait_recv()
    local = pltpu.make_async_copy(peer_wanted, peer_wanted_s, misc_sem.at[2])
    local.start()
    local.wait()

    def main(g):
        @pl.when(g + 1 < groups)
        def _():
            forward(g + 1)

        take_column(g)
        serve_peer(g)

        @pl.when(g > 0)
        def _():
            take_peer(g - 1)
            compute(g - 1)

    loop(groups, main)
    take_peer(groups - 1)
    compute(groups - 1)

    wanted_copy.wait_send()

    def drain(g):
        def body(l):
            @pl.when(has_above)
            def _():
                up(l, g).wait_send()

            aside(l, g, core).wait_send()
            across(l, g).wait_send()

        loop(level + 1, body)
        out_copy(g).wait()

    loop(groups, drain)


def local(queries, key_rows, value_rows, compressed, chosen):
    _, tok_rows, heads_local, groups, head_width = queries.shape
    block_len = BLOCK
    shards = lax.axis_size("seq")
    seq_rank = lax.axis_index("seq")
    blk_dev = tok_rows // block_len
    nblk = blk_dev * shards
    levels = shards // (COLS * CORES)
    rows = block_len * heads_local

    pick_rows = chosen[0]
    all_blocks = jnp.arange(nblk, dtype=jnp.int32)
    onehot = pick_rows[..., None] == all_blocks
    needed = jnp.any(onehot, axis=(0, 2))
    owner_of = all_blocks // blk_dev
    own_col = (seq_rank // CORES) % COLS
    in_column = (owner_of // CORES) % COLS == own_col
    needed_grid = needed.reshape(groups, shards, blk_dev).astype(jnp.int32)
    rank_in = jnp.cumsum(needed_grid, axis=2) - needed_grid
    places = jnp.arange(CAP, dtype=jnp.int32)
    within = jnp.arange(blk_dev, dtype=jnp.int32)
    matched = (needed_grid[..., None] == 1) & (rank_in[..., None] == places)
    wanted = jnp.sum(jnp.where(matched, within[:, None], 0), axis=2)
    wanted = wanted.reshape(groups, shards * CAP)
    wanted = jnp.pad(wanted, ((0, 0), (0, -shards * CAP % 128)))
    pair = owner_of // (COLS * CORES) * CORES + owner_of % CORES
    slot_column = pair * blk_dev + all_blocks % blk_dev
    slot_peer = levels * CORES * blk_dev + pair[None, :] * CAP + rank_in.reshape(groups, nblk)
    slot_of = jnp.where(in_column[None, :], slot_column[None, :], slot_peer)
    pool_index = jnp.sum(jnp.where(onehot, slot_of[None, :, None, :], 0), axis=3)

    key_local = key_rows[0].reshape(tok_rows, groups, head_width)
    value_local = value_rows[0].reshape(tok_rows, groups, head_width)
    own_rows = jnp.transpose(jnp.concatenate([key_local, value_local], axis=-1), (1, 0, 2))
    keys = jnp.transpose(compressed[0], (1, 0, 2))
    pad_rows = 16 * -(-blk_dev // 16)
    extra = jnp.pad(keys, ((0, 0), (0, pad_rows - blk_dev), (0, head_width)))
    own_rows = jnp.concatenate([own_rows, extra], axis=1)
    query_tiles = jnp.transpose(
        queries[0].reshape(blk_dev, rows, groups, head_width), (2, 0, 1, 3)
    )
    shape = (levels, groups, blk_dev, heads_local, block_len, head_width)
    wide = 2 * head_width
    chunk = tok_rows + pad_rows
    served = CORES * CAP * block_len + CORES * blk_dev
    dma = pltpu.SemaphoreType.DMA
    smem = pl.BlockSpec(memory_space=pltpu.SMEM)
    vmem = pl.BlockSpec(memory_space=pltpu.VMEM)
    anyspace = pl.BlockSpec(memory_space=pl.ANY)
    slots = levels * CORES * (blk_dev + CAP)
    bf16 = jnp.bfloat16
    attended, pooled = pl.pallas_call(
        functools.partial(mega, shape),
        in_specs=[smem, smem, vmem, anyspace, anyspace],
        out_specs=[anyspace, vmem],
        out_shape=[
            jax.ShapeDtypeStruct((groups, blk_dev, rows, head_width), bf16),
            jax.ShapeDtypeStruct((blk_dev * groups, nblk), jnp.float32),
        ],
        scratch_shapes=[
            pltpu.VMEM((levels, CORES, groups, chunk, wide), bf16),
            pltpu.VMEM((groups, levels, served, wide), bf16),
            pltpu.VMEM((groups, levels, served, wide), bf16),
            pltpu.VMEM((2, slots, block_len, wide), bf16),
            pltpu.VMEM((2, shards, blk_dev, head_width), jnp.float32),
            pltpu.VMEM((groups, blk_dev, rows, head_width), bf16),
            pltpu.VMEM((groups, blk_dev, rows, head_width), bf16),
            pltpu.VMEM((TOPN * block_len, wide), bf16),
            pltpu.VMEM(wanted.shape, jnp.int32),
            pltpu.SMEM(wanted.shape, jnp.int32),
        ]
        + [dma((levels, groups))] * 6
        + [dma((groups,))] * 3
        + [dma((3,))],
        compiler_params=pltpu.CompilerParams(
            collective_id=0, has_side_effects=True, vmem_limit_bytes=67043328
        ),
    )(pool_index, pick_rows, wanted, own_rows, query_tiles)
    pooled = pooled.reshape(1, blk_dev, groups, nblk)
    shared = lax.psum_scatter(pooled, "head", scatter_dimension=2, tiled=True)
    tile_ids = seq_rank * blk_dev + jnp.arange(blk_dev, dtype=jnp.int32)
    factor = (tile_ids + 1).astype(jnp.float32) / (block_len * HPG)
    block_scores = shared * factor[None, :, None, None]
    attended = jnp.transpose(attended, (1, 2, 0, 3))
    attended = attended.reshape(1, tok_rows, heads_local, groups, head_width)
    return (block_scores, attended)


def solution(mesh):
    placed = (
        P("batch", "seq", "head", None, None),
        P("batch", "seq", None, None),
        P("batch", "seq", None, None),
        P("batch", "seq", None, None),
        P("batch", "seq", None, None),
    )
    return jax.shard_map(
        local,
        mesh=mesh,
        in_specs=placed,
        out_specs=(P("batch", "seq", "head", None), P("batch", "seq", "head", None, None)),
        check_vma=False,
    )
```

time: 340 us -> 218 us (0.64)
  the two profiles are of different devices: /device:TPU:11 before, /device:TPU:24 now
where the time goes in v1:
time: 218 us; the launch traced here: 217 us
  Pallas kernels  180 us (83%)
  local copies, waits for them, and re-layouts  28.1 us (13%)
  other arithmetic  8.82 us (4%)
    pallas_call x1, Pallas kernels, local(): pl.pallas_call(functools.partial(mega, shape), in_specs=[smem, smem, vmem...  180 us
    unnamed x3, local copies, waits for them, and re-layouts  25.1 us

profile of v1, /device:TPU:24, one launch (start us, length us, event | category | flops | bytes accessed | tf_op | source)
XLA Modules:
  0.0 217.4 jit_solution(10284616133365334398)
XLA Ops:
  0.7 0.5 convert_multiply_fusion
  1.2 1.0 fusion.2
  2.2 0.7 copy.30
  2.9 0.1 reshape.189
  3.0 0.1 copy.18
  3.1 1.3 reduce_window_sum.13
  4.4 0.1 reduce_window_sum.14
  4.5 0.1 copy.19
  4.7 0.1 copy.20
  4.8 0.1 copy.21
  4.8 0.6 pad.8.wanted_ref
  5.4 2.7 %select_reduce_fusion.slot_ref = s32[8,8,16]{2,1,0:T(8,128)} fusion(s32[8,128]{1,0:T(8,128)S(1)} %add_select_fusion, s32[8,8,16]{2,1,0:T(8,128)} %bitcast.24), kind=kLoop, calls=%fused_computation.6 | loop fusion | flops 392192 | bytes 12288 | tf_op jit(solution)/shard_map/reduce_sum | solution.py:312
  8.1 1.9 copy_bitcast_fusion
  10.0 0.3 maximum_bitcast_fusion
  10.3 1.5 fusion.1.own_ref
  11.8 7.9 %copy.25 = bf16[1,512,8,8,128]{4,2,1,3,0:T(8,128)(2,1)} copy(bf16[1,512,8,8,128]{4,3,2,1,0:T(8,128)(2,1)} %param.5) | data formatting | bytes 16777216 | tf_op args[0]
  19.7 179.7 %shard_map.68 = (bf16[8,8,512,128]{3,2,1,0:T(8,128)(2,1)}, f32[64,128]{1,0:T(8,128)}) custom-call(s32[8,8,16]{2,1,0:T(8,128)} %select_reduce_fusion.slot_ref, s32[8,8,16]{2,1,0:T(8,128)} %bitcast.25, s32[8,128]{1,0:T(8,128)} %pad.8.wanted_ref, bf16[8,528,256]{2,1,0:T(8,128)(2,1)} %fusion.1.own_ref, bf16[8,8,512,128]{3,2,1,0:T(8,128)(2,1)} %bitcast.21), custom_call_target="tpu_custom_call" | custom-call | tf_op jit(solution)/shard_map/pallas_call | solution.py:334
  199.4 1.5 bitcast_multiply_fusion
  200.9 16.5 %copy.26 = bf16[1,512,8,8,128]{4,3,2,1,0:T(8,128)(2,1)} copy(bf16[1,512,8,8,128]{4,2,1,3,0:T(8,128)(2,1)} %bitcast.22) | data formatting | bytes 16777216
  (7 shorter events, 0.1 us)

commit v2 on v1

v2 whole, which is shorter than its diff:
```python
import functools
import math

import jax
import jax.numpy as jnp
from jax import lax
from jax.experimental import pallas as pl
from jax.experimental.pallas import tpu as pltpu
from jax.sharding import PartitionSpec as P

HPG = 8
BLOCK = 64
TOPN = 16
CAP = 2
COLS = 2
CORES = 2
MESH = pl.DeviceIdType.MESH


def mega(
    shape,
    pick_ref,
    chosen_ref,
    summary_ref,
    key_ref,
    value_ref,
    query_ref,
    out_ref,
    pooled_ref,
    column,
    peer_out,
    peer_in,
    cur,
    summaries,
    summaries_wide,
    queries,
    wide_out,
    stage,
    rows_stage,
    key_part,
    value_part,
    scores_part,
    token_hot,
    mask_bank,
    slot_map,
    slot_map_s,
    wanted,
    peer_wanted,
    peer_wanted_s,
    up_send,
    up_recv,
    sib_send,
    sib_recv,
    peer_send,
    peer_recv,
    key_send,
    key_recv,
    stage_sem,
    misc_sem,
):
    levels, groups, blk_dev, heads_local, block_len, head_width = shape
    rows = block_len * heads_local
    per_level = COLS * CORES
    slots_col = levels * CORES * blk_dev
    picks = CORES * CAP
    f32, bf16 = jnp.float32, jnp.bfloat16

    rank = lax.axis_index("seq")
    core = lax.rem(rank, CORES)
    col = lax.rem(rank // CORES, COLS)
    level = rank // per_level
    sibling = rank + 1 - 2 * core
    peer = rank + CORES * (1 - 2 * col)
    above = rank + per_level
    has_above = level < levels - 1

    def loop(n, body, start=0):
        def step(i, carry):
            body(i)
            return carry

        lax.fori_loop(start, n, step, 0)

    barrier = pltpu.get_barrier_semaphore()
    for other in (sibling, peer):
        pl.semaphore_signal(barrier, inc=1, device_id={"seq": other}, device_id_type=MESH)
    for step in range(1, levels):
        other = lax.rem(rank + step * per_level, levels * per_level)
        pl.semaphore_signal(barrier, inc=1, device_id={"seq": other}, device_id_type=MESH)

    def query_copy(t):
        half = lax.rem(t, 2)
        return pltpu.make_async_copy(query_ref.at[t], stage.at[half], stage_sem.at[half])

    def out_copy(t):
        half = lax.rem(t, 2)
        return pltpu.make_async_copy(stage.at[half], out_ref.at[t], stage_sem.at[half])

    def remote(src, dst, send, recv, device):
        return pltpu.make_async_remote_copy(
            src, dst, send, recv, device_id={"seq": device}, device_id_type=MESH
        )

    def up(l, g):
        part = column.at[l, core, g]
        return remote(part, part, up_send.at[l, g], up_recv.at[l, g], above)

    def aside(l, g, owner):
        part = column.at[l, owner, g]
        return remote(part, part, sib_send.at[l, g], sib_recv.at[l, g], sibling)

    def across(l, g):
        return remote(peer_out.at[g, l], peer_in.at[g, l], peer_send.at[l, g], peer_recv.at[l, g], peer)

    def keys_up(l, source):
        part = summaries.at[source, col, core]
        return remote(part, part, key_send.at[0, l], key_recv.at[0, source], rank + (l - level) * per_level)

    def keys_aside(l, owner):
        part = summaries.at[l, col, owner]
        return remote(part, part, key_send.at[1, l], key_recv.at[1, l], sibling)

    def keys_across(l, owner):
        part = summaries.at[l, owner]
        return remote(part, part, key_send.at[2, l], key_recv.at[2, l], peer)

    wanted_copy = remote(wanted, peer_wanted, misc_sem.at[0], misc_sem.at[1], peer)
    slots_copy = pltpu.make_async_copy(slot_map, slot_map_s, misc_sem.at[2])
    loads = [
        pltpu.make_async_copy(key_ref, rows_stage.at[0], misc_sem.at[4]),
        pltpu.make_async_copy(value_ref, rows_stage.at[1], misc_sem.at[5]),
    ]
    for load in loads:
        load.start()
    query_copy(0).start()

    nblk = levels * per_level * blk_dev
    number = lax.broadcasted_iota(jnp.int32, (groups, nblk), 1)
    named = jnp.zeros((groups, nblk), jnp.int32)
    for t in range(blk_dev):
        picks_here = chosen_ref[t]
        for place in range(TOPN):
            named = jnp.where(picks_here[:, place : place + 1] == number, 1, named)
    inside = lax.rem(number, blk_dev)
    order = named
    step = 1
    while step < blk_dev:
        order = order + jnp.where(inside >= step, pltpu.roll(order, step, 1), 0)
        step *= 2
    order = order - named
    for k in range(CAP):
        found = jnp.where((named == 1) & (order == k), inside, 0)
        step = 1
        while step < blk_dev:
            found = found + pltpu.roll(found, nblk - step, 1)
            step *= 2
        wanted[k] = found
    device = number // blk_dev
    pair = device // per_level * CORES + lax.rem(device, CORES)
    in_column = lax.rem(device // CORES, COLS) == col
    slot_map[...] = jnp.where(in_column, pair * blk_dev + inside, slots_col + pair * CAP + order)

    own_summary = jnp.swapaxes(summary_ref[...].astype(f32), 0, 1)
    own_summary = own_summary.reshape(groups * blk_dev, head_width).astype(bf16)
    summaries[level, col, core] = own_summary
    row_token = lax.broadcasted_iota(jnp.int32, (rows, head_width), 0) // heads_local
    row_lane = lax.broadcasted_iota(jnp.int32, (rows, head_width), 1)
    token_hot[...] = jnp.where(row_token == row_lane, 1.0, 0.0).astype(bf16)
    key_place = lax.broadcasted_iota(jnp.int32, (block_len, head_width), 0)
    key_lane = lax.broadcasted_iota(jnp.int32, (block_len, head_width), 1)
    mask_bank[0] = jnp.zeros((block_len, head_width), bf16)
    mask_bank[1] = jnp.where(key_place > key_lane, -1e30, 0.0).astype(bf16)
    value_part[:, head_width:] = jnp.ones((TOPN * block_len, head_width), bf16)
    summaries_wide[...] = jnp.zeros_like(summaries_wide)
    for kind in range(2):
        loads[kind].wait()

        def split(r, kind=kind):
            here = pl.ds(pl.multiple_of(r * block_len, block_len), block_len)
            apart = jnp.swapaxes(rows_stage[kind, here].astype(f32), 0, 1).astype(bf16)
            for g in range(groups):
                column[level, core, g, here, kind * head_width : (kind + 1) * head_width] = apart[g]

        loop(blk_dev, split)
    slots_copy.start()
    pl.semaphore_wait(barrier, levels + 1)

    loop(levels, lambda l: keys_up(l, level).start(), level + 1)
    keys_aside(level, core).start()
    wanted_copy.start()

    def send_own(g):
        @pl.when(has_above)
        def _():
            up(level, g).start()

    lead = 3
    for g in range(min(lead, groups - 1)):
        send_own(g)
    loop(groups, lambda g: aside(level, g, core).start())

    def spread(t):
        query_copy(t).wait()

        @pl.when(t + 1 < blk_dev)
        def _():
            query_copy(t + 1).start()

        half = lax.rem(t, 2)
        wide_out[t] = stage[half].astype(f32).reshape(rows * groups, head_width)
        for g in range(groups):
            queries[g, t] = wide_out[t, pl.ds(g, rows, stride=groups)].astype(bf16)

    loop(blk_dev, spread)

    def relay_keys(l):
        keys_up(l, l).wait_recv()
        keys_aside(l, core).start()

    def pair_keys(l):
        keys_aside(l, 1 - core).wait_recv()
        keys_across(l, col).start()

    def widen_keys(l):
        keys_across(l, 1 - col).wait_recv()
        for x in range(COLS):
            for c in range(CORES):
                summaries_wide[(l * COLS + x) * CORES + c] = summaries[l, x, c].astype(f32)

    loop(level, relay_keys)
    loop(level + 1, pair_keys)
    wanted_copy.wait_recv()
    local_wanted = pltpu.make_async_copy(peer_wanted, peer_wanted_s, misc_sem.at[3])
    local_wanted.start()
    local_wanted.wait()
    slots_copy.wait()
    loop(level + 1, widen_keys)

    def relay(g, l):
        up(l, g).wait_recv()

        @pl.when(has_above)
        def _():
            up(l, g).start()

        aside(l, g, core).start()

    def take(g, l):
        half = lax.rem(g, 2)
        aside(l, g, 1 - core).wait_recv()
        for c in range(CORES):
            first = (l * CORES + c) * blk_dev
            for b in range(blk_dev):
                cur[half, first + b] = column[l, c, g, b * block_len : (b + 1) * block_len]
        for c in range(CORES):
            source = (l * COLS + col) * CORES + c
            for k in range(CAP):
                index = peer_wanted_s[k, g, source * blk_dev]
                place = (c * CAP + k) * block_len
                peer_out[g, l, place : place + block_len] = cur[half, (l * CORES + c) * blk_dev + index]
        across(l, g).start()

    def take_peer(g):
        half = lax.rem(g, 2)

        def body(i):
            l = level - i
            across(l, g).wait_recv()
            for k in range(picks):
                cur[half, slots_col + l * picks + k] = peer_in[g, l, k * block_len : (k + 1) * block_len]

        loop(level + 1, body)

    factor = math.log2(math.e) * head_width ** (-0.5)
    part = min(rows, 256)
    parts = rows // part
    across_lanes = (((1,), (1,)), ((), ()))

    def score_tile(t, first_group, groups_end):
        tile_number = rank * blk_dev + t
        seen = lax.broadcasted_iota(jnp.int32, (1, nblk), 1) <= tile_number

        def body(g):
            first = pl.multiple_of(g * blk_dev, blk_dev)
            summary = summaries_wide[:, pl.ds(first, blk_dev)].reshape(nblk, head_width).astype(bf16)
            logits = lax.dot_general(queries[g, t], summary, across_lanes, preferred_element_type=f32)
            logits = jnp.where(seen, logits, -jnp.inf)
            top = jnp.max(logits, axis=-1, keepdims=True)
            weights = jnp.exp2((logits - top) * factor)
            totals = jnp.sum(weights, axis=-1, keepdims=True)
            pooled = jnp.sum(weights / totals, axis=0, keepdims=True)
            pooled_ref[pl.ds(t * groups + g, 1), :] = pooled

        loop(groups_end, body, first_group)

    def attend(g, t):
        half = lax.rem(g, 2)
        tile_number = rank * blk_dev + t
        for place in range(TOPN):
            here = slice(place * block_len, (place + 1) * block_len)
            number_here = pick_ref[t, g, place]
            slot = slot_map_s[g, number_here]
            is_own = (number_here == tile_number).astype(jnp.int32)
            key_part[here, :head_width] = cur[half, slot, :, :head_width]
            key_part[here, head_width:] = mask_bank[is_own]
            value_part[here, :head_width] = cur[half, slot, :, head_width:]

        def score(i):
            here = pl.ds(i * part, part)
            query = jnp.concatenate([queries[g, t, here], token_hot[here]], axis=1)
            scores_part[i % 2] = lax.dot_general(
                query, key_part[...], across_lanes, preferred_element_type=f32
            )

        score(0)
        for i in range(parts):
            if i + 1 < parts:
                score(i + 1)
            scores = scores_part[i % 2]
            top = jnp.max(scores, axis=-1, keepdims=True)
            weights = jnp.exp2((scores - top) * factor).astype(bf16)
            mixed = jnp.dot(weights, value_part[...], preferred_element_type=f32)
            result = mixed[:, :head_width] / mixed[:, head_width:]
            wide_out[t, pl.ds(i * part * groups + g, part, stride=groups)] = result

    relay_at = [0] + [(i - 1) * blk_dev // max(levels - 2, 1) for i in range(1, levels)]
    take_at = [0] + [min(spot + 1, blk_dev) for spot in relay_at[1:]]

    def relays(g, t, i):
        @pl.when((t == relay_at[i]) & (level >= i))
        def _():
            relay(g, level - i)

    def takes(g, t, i):
        @pl.when((t == take_at[i]) & (level >= i))
        def _():
            take(g, level - i)

    def main(g):
        @pl.when((g > 0) & (g + lead - 1 < groups - 1))
        def _():
            send_own(g + lead - 1)

        @pl.when(g == groups - 1)
        def _():
            send_own(g)

        def tile(t):
            for i in range(levels):
                if i > 0 and relay_at[i] < blk_dev:
                    relays(g, t, i)
                if take_at[i] < blk_dev:
                    takes(g, t, i)

            @pl.when(g > 0)
            def _():
                attend(g - 1, t)

        loop(blk_dev, tile)
        for i in range(1, levels):
            if relay_at[i] == blk_dev:
                relays(g, blk_dev, i)
        first_tile, end_tile = g * blk_dev // groups, (g + 1) * blk_dev // groups
        loop(end_tile, lambda t: score_tile(t, 0, groups // 2), first_tile)
        for i in range(1, levels):
            if take_at[i] == blk_dev:
                takes(g, blk_dev, i)
        loop(end_tile, lambda t: score_tile(t, groups // 2, groups), first_tile)
        take_peer(g)

    loop(groups, main)

    def last(t):
        attend(groups - 1, t)

        @pl.when(t > 1)
        def _():
            out_copy(t - 2).wait()

        stage[lax.rem(t, 2)] = wide_out[t].reshape(rows, groups, head_width).astype(bf16)
        out_copy(t).start()

    loop(blk_dev, last)

    wanted_copy.wait_send()
    loop(levels, lambda l: keys_up(l, level).wait_send(), level + 1)

    def drain_keys(l):
        keys_aside(l, core).wait_send()
        keys_across(l, col).wait_send()

    loop(level + 1, drain_keys)

    def drain(g):
        def body(l):
            @pl.when(has_above)
            def _():
                up(l, g).wait_send()

            aside(l, g, core).wait_send()
            across(l, g).wait_send()

        loop(level + 1, body)

    loop(groups, drain)
    for t in range(max(blk_dev - 2, 0), blk_dev):
        out_copy(t).wait()


def local(queries, key_rows, value_rows, compressed, chosen):
    _, tok_rows, heads_local, groups, head_width = queries.shape
    block_len = BLOCK
    shards = lax.axis_size("seq")
    seq_rank = lax.axis_index("seq")
    blk_dev = tok_rows // block_len
    nblk = blk_dev * shards
    levels = shards // (COLS * CORES)
    rows = block_len * heads_local

    pick_rows = chosen[0]
    query_tiles = queries[0].reshape(blk_dev, rows, groups, head_width)
    shape = (levels, groups, blk_dev, heads_local, block_len, head_width)
    wide = 2 * head_width
    served = CORES * CAP * block_len
    part = min(rows, 256)
    dma = pltpu.SemaphoreType.DMA
    smem = pl.BlockSpec(memory_space=pltpu.SMEM)
    vmem = pl.BlockSpec(memory_space=pltpu.VMEM)
    anyspace = pl.BlockSpec(memory_space=pl.ANY)
    slots = levels * CORES * (blk_dev + CAP)
    bf16, f32 = jnp.bfloat16, jnp.float32
    attended, pooled = pl.pallas_call(
        functools.partial(mega, shape),
        in_specs=[smem, vmem, vmem, anyspace, anyspace, anyspace],
        out_specs=[anyspace, vmem],
        out_shape=[
            jax.ShapeDtypeStruct((blk_dev, rows, groups, head_width), bf16),
            jax.ShapeDtypeStruct((blk_dev * groups, nblk), f32),
        ],
        scratch_shapes=[
            pltpu.VMEM((levels, CORES, groups, tok_rows, wide), bf16),
            pltpu.VMEM((groups, levels, served, wide), bf16),
            pltpu.VMEM((groups, levels, served, wide), bf16),
            pltpu.VMEM((2, slots, block_len, wide), bf16),
            pltpu.VMEM((levels, COLS, CORES, groups * blk_dev, head_width), bf16),
            pltpu.VMEM((shards, groups * blk_dev, head_width), f32),
            pltpu.VMEM((groups, blk_dev, rows, head_width), bf16),
            pltpu.VMEM((blk_dev, rows * groups, head_width), f32),
            pltpu.VMEM((2, rows, groups, head_width), bf16),
            pltpu.VMEM((2, tok_rows, groups, head_width), bf16),
            pltpu.VMEM((TOPN * block_len, wide), bf16),
            pltpu.VMEM((TOPN * block_len, wide), bf16),
            pltpu.VMEM((2, part, TOPN * block_len), f32),
            pltpu.VMEM((rows, head_width), bf16),
            pltpu.VMEM((2, block_len, head_width), bf16),
            pltpu.VMEM((groups, nblk), jnp.int32),
            pltpu.SMEM((groups, nblk), jnp.int32),
            pltpu.VMEM((CAP, groups, nblk), jnp.int32),
            pltpu.VMEM((CAP, groups, nblk), jnp.int32),
            pltpu.SMEM((CAP, groups, nblk), jnp.int32),
        ]
        + [dma((levels, groups))] * 6
        + [dma((3, levels))] * 2
        + [dma((2,)), dma((6,))],
        compiler_params=pltpu.CompilerParams(
            collective_id=0, has_side_effects=True, vmem_limit_bytes=67043328
        ),
    )(pick_rows, pick_rows, compressed[0], key_rows[0], value_rows[0], query_tiles)
    pooled = pooled.reshape(1, blk_dev, groups, nblk)
    shared = lax.psum_scatter(pooled, "head", scatter_dimension=2, tiled=True)
    tile_ids = seq_rank * blk_dev + jnp.arange(blk_dev, dtype=jnp.int32)
    factor = (tile_ids + 1).astype(jnp.float32) / (block_len * HPG)
    block_scores = shared * factor[None, :, None, None]
    attended = attended.reshape(1, tok_rows, heads_local, groups, head_width)
    return (block_scores, attended)


def solution(mesh):
    placed = (
        P("batch", "seq", "head", None, None),
        P("batch", "seq", None, None),
        P("batch", "seq", None, None),
        P("batch", "seq", None, None),
        P("batch", "seq", None, None),
    )
    return jax.shard_map(
        local,
        mesh=mesh,
        in_specs=placed,
        out_specs=(P("batch", "seq", "head", None), P("batch", "seq", "head", None, None)),
        check_vma=False,
    )
```

time: 218 us -> 184 us (0.84)
  local copies, waits for them, and re-layouts: 28.1 us -> 8.81 us
  Pallas kernels: 180 us -> 172 us
  other arithmetic: 8.82 us -> 1.97 us
    unnamed x3 -> x1, local copies, waits for them, and re-layouts: 25.1 us -> 8.81 us
    pallas_call x1, Pallas kernels: 180 us -> 172 us  [local(): pl.pallas_call(functools.partial(mega, shape), in_specs=[smem, vmem, vmem...]
    reduce_sum x2 -> x0, other arithmetic: 2.73 us -> none  [the longest x1 2.68 us: local(): jnp.sum(jnp.where(onehot, slot_of[None, :, None, :], 0), axis=3)]
where the time goes in v2:
time: 184 us; the launch traced here: 183 us
  Pallas kernels  172 us (93%)
  local copies, waits for them, and re-layouts  8.81 us (5%)
  other arithmetic  1.97 us (1%)
    pallas_call x1, Pallas kernels, local(): pl.pallas_call(functools.partial(mega, shape), in_specs=[smem, vmem, vmem...  172 us
    unnamed x1, local copies, waits for them, and re-layouts  8.81 us

profile of v2, /device:TPU:24, one launch (start us, length us, event | category | flops | bytes accessed | tf_op | source)
XLA Modules:
  0.0 183.1 jit_solution(12314950788157743189)
XLA Ops:
  0.6 0.5 convert_multiply_fusion
  1.2 171.7 %shard_map.68 = (bf16[8,512,8,128]{3,2,1,0:T(8,128)(2,1)}, f32[64,128]{1,0:T(8,128)}) custom-call(s32[8,8,16]{2,1,0:T(8,128)} %bitcast.12, s32[8,8,16]{2,1,0:T(8,128)} %bitcast.13, bf16[8,8,128]{2,1,0:T(8,128)(2,1)} %bitcast.14, bf16[512,8,128]{2,1,0:T(8,128)(2,1)} %bitcast.10, bf16[512,8,128]{2,1,0:T(8,128)(2,1)} %bitcast.11, bf16[8,512,8,128]{3,2,1,0:T(8,128)(2,1)} %bitcast.8), custom_call_target="tpu_custom_call" | custom-call | tf_op jit(solution)/shard_map/pallas_call | solution.py:432
  172.9 1.5 bitcast_multiply_fusion
  174.3 8.8 %copy.8 = bf16[1,512,8,8,128]{4,3,2,1,0:T(8,128)(2,1)} copy(bf16[1,512,8,8,128]{4,3,2,1,0:T(8,128)(2,1)} %bitcast.9) | data formatting | bytes 16777216

commit v3 on v2

--- a/solution.py
+++ b/solution.py
@@ -15,6 +15,102 @@
 COLS = 2
 CORES = 2
 MESH = pl.DeviceIdType.MESH
+
+
+def prepare(shape, token_hot, mask_bank, value_part):
+    _, _, _, heads_local, block_len, head_width = shape
+    rows = block_len * heads_local
+    row_token = lax.broadcasted_iota(jnp.int32, (rows, head_width), 0) // heads_local
+    row_lane = lax.broadcasted_iota(jnp.int32, (rows, head_width), 1)
+    token_hot[...] = jnp.where(row_token == row_lane, 1.0, 0.0).astype(jnp.bfloat16)
+    key_place = lax.broadcasted_iota(jnp.int32, (block_len, head_width), 0)
+    key_lane = lax.broadcasted_iota(jnp.int32, (block_len, head_width), 1)
+    mask_bank[0] = jnp.zeros((block_len, head_width), jnp.bfloat16)
+    mask_bank[1] = jnp.where(key_place > key_lane, -1e30, 0.0).astype(jnp.bfloat16)
+    value_part[:, head_width:] = jnp.ones((TOPN * block_len, head_width), jnp.bfloat16)
+
+
+def attend_unit(shape, pool, number_at, slot_at, tile_number, query_at, store, work):
+    _, _, _, heads_local, block_len, head_width = shape
+    key_part, value_part, scores_part, token_hot, mask_bank = work
+    rows = block_len * heads_local
+    part = min(rows, 256)
+    parts = rows // part
+    factor = math.log2(math.e) * head_width ** (-0.5)
+    for place in range(TOPN):
+        here = slice(place * block_len, (place + 1) * block_len)
+        number = number_at(place)
+        slot = slot_at(number)
+        is_own = (number == tile_number).astype(jnp.int32)
+        key_part[here, :head_width] = pool[slot, :, :head_width]
+        key_part[here, head_width:] = mask_bank[is_own]
+        value_part[here, :head_width] = pool[slot, :, head_width:]
+
+    def score(i):
+        here = pl.ds(i * part, part)
+        query = jnp.concatenate([query_at(here), token_hot[here]], axis=1)
+        scores_part[i % 2] = lax.dot_general(
+            query, key_part[...], (((1,), (1,)), ((), ())), preferred_element_type=jnp.float32
+        )
+
+    score(0)
+    for i in range(parts):
+        if i + 1 < parts:
+            score(i + 1)
+        scores = scores_part[i % 2]
+        top = jnp.max(scores, axis=-1, keepdims=True)
+        weights = jnp.exp2((scores - top) * factor).astype(jnp.bfloat16)
+        mixed = jnp.dot(weights, value_part[...], preferred_element_type=jnp.float32)
+        store(i * part, part, mixed[:, :head_width] / mixed[:, head_width:])
+
+
+def finish(
+    shape,
+    pick_ref,
+    slot_ref,
+    partial_ref,
+    query_ref,
+    pool_ref,
+    pooled_ref,
+    out_ref,
+    block_scores_ref,
+    wide,
+    key_part,
+    value_part,
+    scores_part,
+    token_hot,
+    mask_bank,
+):
+    _, groups, blk_dev, heads_local, block_len, head_width = shape
+    rows = block_len * heads_local
+    rank = lax.axis_index("seq")
+    t = pl.program_id(0)
+    last = groups - 1
+
+    @pl.when(t == 0)
+    def _():
+        prepare(shape, token_hot, mask_bank, value_part)
+        lines = pooled_ref.shape[0]
+        line_tile = lax.broadcasted_iota(jnp.int32, (lines, 1), 0) // (lines // blk_dev)
+        scale = (rank * blk_dev + line_tile + 1).astype(jnp.float32) / (block_len * HPG)
+        block_scores_ref[...] = pooled_ref[...] * scale
+
+    wide[...] = partial_ref[0].astype(jnp.float32).reshape(rows * groups, head_width)
+
+    def store(start, count, result):
+        wide[pl.ds(start * groups + last, count, stride=groups)] = result
+
+    attend_unit(
+        shape,
+        pool_ref,
+        lambda place: pick_ref[t, last, place],
+        lambda number: slot_ref[last, number],
+        rank * blk_dev + t,
+        lambda here: query_ref[0, here],
+        store,
+        (key_part, value_part, scores_part, token_hot, mask_bank),
+    )
+    out_ref[0] = wide[...].reshape(rows, groups, head_width).astype(jnp.bfloat16)
 
 
 def mega(
@@ -27,6 +123,9 @@
     query_ref,
     out_ref,
     pooled_ref,
+    pool_out,
+    query_out,
+    slot_out,
     column,
     peer_out,
     peer_in,
@@ -56,6 +155,7 @@
     key_send,
     key_recv,
     stage_sem,
+    pool_sem,
     misc_sem,
 ):
     levels, groups, blk_dev, heads_local, block_len, head_width = shape
@@ -163,14 +263,7 @@
     own_summary = jnp.swapaxes(summary_ref[...].astype(f32), 0, 1)
     own_summary = own_summary.reshape(groups * blk_dev, head_width).astype(bf16)
     summaries[level, col, core] = own_summary
-    row_token = lax.broadcasted_iota(jnp.int32, (rows, head_width), 0) // heads_local
-    row_lane = lax.broadcasted_iota(jnp.int32, (rows, head_width), 1)
-    token_hot[...] = jnp.where(row_token == row_lane, 1.0, 0.0).astype(bf16)
-    key_place = lax.broadcasted_iota(jnp.int32, (block_len, head_width), 0)
-    key_lane = lax.broadcasted_iota(jnp.int32, (block_len, head_width), 1)
-    mask_bank[0] = jnp.zeros((block_len, head_width), bf16)
-    mask_bank[1] = jnp.where(key_place > key_lane, -1e30, 0.0).astype(bf16)
-    value_part[:, head_width:] = jnp.ones((TOPN * block_len, head_width), bf16)
+    prepare(shape, token_hot, mask_bank, value_part)
     summaries_wide[...] = jnp.zeros_like(summaries_wide)
     for kind in range(2):
         loads[kind].wait()
@@ -194,9 +287,8 @@
         def _():
             up(level, g).start()
 
-    lead = 3
-    for g in range(min(lead, groups - 1)):
-        send_own(g)
+    lead = jnp.where(level == 0, groups, jnp.where(level == levels - 2, min(3, groups), 1))
+    loop(lead, send_own)
     loop(groups, lambda g: aside(level, g, core).start())
 
     def spread(t):
@@ -212,6 +304,12 @@
             queries[g, t] = wide_out[t, pl.ds(g, rows, stride=groups)].astype(bf16)
 
     loop(blk_dev, spread)
+    handed_on = [
+        pltpu.make_async_copy(queries.at[groups - 1], query_out, misc_sem.at[6]),
+        pltpu.make_async_copy(slot_map, slot_out, misc_sem.at[7]),
+    ]
+    for copy in handed_on:
+        copy.start()
 
     def relay_keys(l):
         keys_up(l, l).wait_recv()
@@ -260,6 +358,10 @@
                 peer_out[g, l, place : place + block_len] = cur[half, (l * CORES + c) * blk_dev + index]
         across(l, g).start()
 
+        @pl.when(g == groups - 1)
+        def _():
+            pool_copy(0, l).start()
+
     def take_peer(g):
         half = lax.rem(g, 2)
 
@@ -269,11 +371,13 @@
             for k in range(picks):
                 cur[half, slots_col + l * picks + k] = peer_in[g, l, k * block_len : (k + 1) * block_len]
 
+            @pl.when(g == groups - 1)
+            def _():
+                pool_copy(1, l).start()
+
         loop(level + 1, body)
 
     factor = math.log2(math.e) * head_width ** (-0.5)
-    part = min(rows, 256)
-    parts = rows // part
     across_lanes = (((1,), (1,)), ((), ()))
 
     def score_tile(t, first_group, groups_end):
@@ -295,35 +399,35 @@
 
     def attend(g, t):
         half = lax.rem(g, 2)
-        tile_number = rank * blk_dev + t
-        for place in range(TOPN):
-            here = slice(place * block_len, (place + 1) * block_len)
-            number_here = pick_ref[t, g, place]
-            slot = slot_map_s[g, number_here]
-            is_own = (number_here == tile_number).astype(jnp.int32)
-            key_part[here, :head_width] = cur[half, slot, :, :head_width]
-            key_part[here, head_width:] = mask_bank[is_own]
-            value_part[here, :head_width] = cur[half, slot, :, head_width:]
-
-        def score(i):
-            here = pl.ds(i * part, part)
-            query = jnp.concatenate([queries[g, t, here], token_hot[here]], axis=1)
-            scores_part[i % 2] = lax.dot_general(
-                query, key_part[...], across_lanes, preferred_element_type=f32
-            )
-
-        score(0)
-        for i in range(parts):
-            if i + 1 < parts:
-                score(i + 1)
-            scores = scores_part[i % 2]
-            top = jnp.max(scores, axis=-1, keepdims=True)
-            weights = jnp.exp2((scores - top) * factor).astype(bf16)
-            mixed = jnp.dot(weights, value_part[...], preferred_element_type=f32)
-            result = mixed[:, :head_width] / mixed[:, head_width:]
-            wide_out[t, pl.ds(i * part * groups + g, part, stride=groups)] = result
-
-    relay_at = [0] + [(i - 1) * blk_dev // max(levels - 2, 1) for i in range(1, levels)]
+
+        def store(start, count, result):
+            wide_out[t, pl.ds(start * groups + g, count, stride=groups)] = result
+
+        attend_unit(
+            shape,
+            cur.at[half],
+            lambda place: pick_ref[t, g, place],
+            lambda number: slot_map_s[g, number],
+            rank * blk_dev + t,
+            lambda here: queries[g, t, here],
+            store,
+            (key_part, value_part, scores_part, token_hot, mask_bank),
+        )
+
+    def put_out(t):
+        @pl.when(t > 1)
+        def _():
+            out_copy(t - 2).wait()
+
+        stage[lax.rem(t, 2)] = wide_out[t].reshape(rows, groups, head_width).astype(bf16)
+        out_copy(t).start()
+
+    def pool_copy(kind, l):
+        count = (CORES * blk_dev, picks)[kind]
+        here = pl.ds(kind * slots_col + l * count, count)
+        return pltpu.make_async_copy(cur.at[(groups - 1) % 2, here], pool_out.at[here], pool_sem.at[kind, l])
+
+    relay_at = [0] + [(i - 1) * (blk_dev - 2) // max(levels - 2, 1) for i in range(1, levels)]
     take_at = [0] + [min(spot + 1, blk_dev) for spot in relay_at[1:]]
 
     def relays(g, t, i):
@@ -331,20 +435,16 @@
         def _():
             relay(g, level - i)
 
+        @pl.when((t == relay_at[i]) & (level == i) & (g + 1 >= lead) & (g + 1 < groups))
+        def _():
+            send_own(g + 1)
+
     def takes(g, t, i):
         @pl.when((t == take_at[i]) & (level >= i))
         def _():
             take(g, level - i)
 
     def main(g):
-        @pl.when((g > 0) & (g + lead - 1 < groups - 1))
-        def _():
-            send_own(g + lead - 1)
-
-        @pl.when(g == groups - 1)
-        def _():
-            send_own(g)
-
         def tile(t):
             for i in range(levels):
                 if i > 0 and relay_at[i] < blk_dev:
@@ -355,6 +455,10 @@
             @pl.when(g > 0)
             def _():
                 attend(g - 1, t)
+
+            @pl.when(g == groups - 1)
+            def _():
+                put_out(t)
 
         loop(blk_dev, tile)
         for i in range(1, levels):
@@ -370,22 +474,12 @@
 
     loop(groups, main)
 
-    def last(t):
-        attend(groups - 1, t)
-
-        @pl.when(t > 1)
-        def _():
-            out_copy(t - 2).wait()
-
-        stage[lax.rem(t, 2)] = wide_out[t].reshape(rows, groups, head_width).astype(bf16)
-        out_copy(t).start()
-
-    loop(blk_dev, last)
-
     wanted_copy.wait_send()
     loop(levels, lambda l: keys_up(l, level).wait_send(), level + 1)
 
     def drain_keys(l):
+        pool_copy(0, l).wait()
+        pool_copy(1, l).wait()
         keys_aside(l, core).wait_send()
         keys_across(l, col).wait_send()
 
@@ -405,13 +499,14 @@
     loop(groups, drain)
     for t in range(max(blk_dev - 2, 0), blk_dev):
         out_copy(t).wait()
+    for copy in handed_on:
+        copy.wait()
 
 
 def local(queries, key_rows, value_rows, compressed, chosen):
     _, tok_rows, heads_local, groups, head_width = queries.shape
     block_len = BLOCK
     shards = lax.axis_size("seq")
-    seq_rank = lax.axis_index("seq")
     blk_dev = tok_rows // block_len
     nblk = blk_dev * shards
     levels = shards // (COLS * CORES)
@@ -429,13 +524,16 @@
     anyspace = pl.BlockSpec(memory_space=pl.ANY)
     slots = levels * CORES * (blk_dev + CAP)
     bf16, f32 = jnp.bfloat16, jnp.float32
-    attended, pooled = pl.pallas_call(
+    partial, pooled, pool, last_queries, slot_map = pl.pallas_call(
         functools.partial(mega, shape),
         in_specs=[smem, vmem, vmem, anyspace, anyspace, anyspace],
-        out_specs=[anyspace, vmem],
+        out_specs=[anyspace, vmem, anyspace, anyspace, anyspace],
         out_shape=[
             jax.ShapeDtypeStruct((blk_dev, rows, groups, head_width), bf16),
             jax.ShapeDtypeStruct((blk_dev * groups, nblk), f32),
+            jax.ShapeDtypeStruct((slots, block_len, wide), bf16),
+            jax.ShapeDtypeStruct((blk_dev, rows, head_width), bf16),
+            jax.ShapeDtypeStruct((groups, nblk), jnp.int32),
         ],
         scratch_shapes=[
             pltpu.VMEM((levels, CORES, groups, tok_rows, wide), bf16),
@@ -461,16 +559,39 @@
         ]
         + [dma((levels, groups))] * 6
         + [dma((3, levels))] * 2
-        + [dma((2,)), dma((6,))],
+        + [dma((2,)), dma((2, levels)), dma((8,))],
         compiler_params=pltpu.CompilerParams(
             collective_id=0, has_side_effects=True, vmem_limit_bytes=67043328
         ),
     )(pick_rows, pick_rows, compressed[0], key_rows[0], value_rows[0], query_tiles)
     pooled = pooled.reshape(1, blk_dev, groups, nblk)
     shared = lax.psum_scatter(pooled, "head", scatter_dimension=2, tiled=True)
-    tile_ids = seq_rank * blk_dev + jnp.arange(blk_dev, dtype=jnp.int32)
-    factor = (tile_ids + 1).astype(jnp.float32) / (block_len * HPG)
-    block_scores = shared * factor[None, :, None, None]
+    groups_out = shared.shape[2]
+    whole = pl.BlockSpec((slots, block_len, wide), lambda t: (0, 0, 0))
+    lines = pl.BlockSpec((blk_dev * groups_out, nblk), lambda t: (0, 0))
+    tile = pl.BlockSpec((1, rows, groups, head_width), lambda t: (t, 0, 0, 0))
+    attended, block_scores = pl.pallas_call(
+        functools.partial(finish, shape),
+        grid=(blk_dev,),
+        in_specs=[smem, smem, tile, pl.BlockSpec((1, rows, head_width), lambda t: (t, 0, 0)), whole, lines],
+        out_specs=[tile, lines],
+        out_shape=[
+            jax.ShapeDtypeStruct((blk_dev, rows, groups, head_width), bf16),
+            jax.ShapeDtypeStruct((blk_dev * groups_out, nblk), f32),
+        ],
+        scratch_shapes=[
+            pltpu.VMEM((rows * groups, head_width), f32),
+            pltpu.VMEM((TOPN * block_len, wide), bf16),
+            pltpu.VMEM((TOPN * block_len, wide), bf16),
+            pltpu.VMEM((2, part, TOPN * block_len), f32),
+            pltpu.VMEM((rows, head_width), bf16),
+            pltpu.VMEM((2, block_len, head_width), bf16),
+        ],
+        compiler_params=pltpu.CompilerParams(
+            dimension_semantics=("arbitrary",), vmem_limit_bytes=67043328
+        ),
+    )(pick_rows, slot_map, partial, last_queries, pool, shared.reshape(blk_dev * groups_out, nblk))
+    block_scores = block_scores.reshape(1, blk_dev, groups_out, nblk)
     attended = attended.reshape(1, tok_rows, heads_local, groups, head_width)
     return (block_scores, attended)
 

time: 184 us -> 170 us (0.924)
  local copies, waits for them, and re-layouts: 8.81 us -> 0 us
  Pallas kernels: 172 us -> 168 us
  other arithmetic: 1.97 us -> 0 us
    pallas_call x1, Pallas kernels: 172 us -> 153 us  [local(): pl.pallas_call(functools.partial(mega, shape), in_specs=[smem, vmem, vmem...]
    pallas_call x0 -> x1, Pallas kernels: none -> 14.5 us  [local(): pl.pallas_call(functools.partial(finish, shape), grid=(blk_dev,), in_spec...]
    unnamed x1 -> x0, local copies, waits for them, and re-layouts: 8.81 us -> none
where the time goes in v3:
time: 170 us; the launch traced here: 168 us
  Pallas kernels  168 us (99%)
    pallas_call x1, Pallas kernels, local(): pl.pallas_call(functools.partial(mega, shape), in_specs=[smem, vmem, vmem...  153 us
    pallas_call x1, Pallas kernels, local(): pl.pallas_call(functools.partial(finish, shape), grid=(blk_dev,), in_spec...  14.5 us

profile of v3, /device:TPU:24, one launch (start us, length us, event | category | flops | bytes accessed | tf_op | source)
XLA Modules:
  0.0 168.4 jit_solution(3357373790990370328)
XLA Ops:
  0.6 153.3 %shard_map.68 = (bf16[8,512,8,128]{3,2,1,0:T(8,128)(2,1)}, f32[64,128]{1,0:T(8,128)}, bf16[80,64,256]{2,1,0:T(8,128)(2,1)}, bf16[8,512,128]{2,1,0:T(8,128)(2,1)}, s32[8,128]{1,0:T(8,128)}) custom-call(s32[8,8,16]{2,1,0:T(8,128)} %bitcast.10, s32[8,8,16]{2,1,0:T(8,128)} %bitcast.11, bf16[8,8,128]{2,1,0:T(8,128)(2,1)} %bitcast.13, ...), custom_call_target="tpu_custom_call" | custom-call | tf_op jit(solution)/shard_map/pallas_call | solution.py:527
  153.9 14.5 %shard_map.69 = (bf16[8,512,8,128]{3,2,1,0:T(8,128)(2,1)}, f32[64,128]{1,0:T(8,128)}) custom-call(s32[8,8,16]{2,1,0:T(8,128)} %bitcast.12, s32[8,128]{1,0:T(8,128)} %get-tuple-element.9.slot_ref, bf16[8,512,8,128]{3,2,1,0:T(8,128)(2,1)} %get-tuple-element.10.partial_ref, bf16[8,512,128]{2,1,0:T(8,128)(2,1)} %get-tuple-element.11.query_ref, ...), custom_call_target="tpu_custom_call" | custom-call | tf_op jit(solution)/shard_map/pallas_call | solution.py:573

commit v4 on v3

--- a/solution.py
+++ b/solution.py
@@ -17,7 +17,7 @@
 MESH = pl.DeviceIdType.MESH
 
 
-def prepare(shape, token_hot, mask_bank, value_part):
+def prepare(shape, token_hot, mask_bank, value_parts):
     _, _, _, heads_local, block_len, head_width = shape
     rows = block_len * heads_local
     row_token = lax.broadcasted_iota(jnp.int32, (rows, head_width), 0) // heads_local
@@ -27,41 +27,54 @@
     key_lane = lax.broadcasted_iota(jnp.int32, (block_len, head_width), 1)
     mask_bank[0] = jnp.zeros((block_len, head_width), jnp.bfloat16)
     mask_bank[1] = jnp.where(key_place > key_lane, -1e30, 0.0).astype(jnp.bfloat16)
-    value_part[:, head_width:] = jnp.ones((TOPN * block_len, head_width), jnp.bfloat16)
-
-
-def attend_unit(shape, pool, number_at, slot_at, tile_number, query_at, store, work):
+    lanes = value_parts.shape[2] - head_width
+    for i in range(value_parts.shape[0]):
+        value_parts[i, :, head_width:] = jnp.ones((TOPN * block_len, lanes), jnp.bfloat16)
+
+
+def attend_units(shape, pool, units, work):
     _, _, _, heads_local, block_len, head_width = shape
-    key_part, value_part, scores_part, token_hot, mask_bank = work
+    key_parts, value_parts, scores_parts, token_hot, mask_bank = work
     rows = block_len * heads_local
     part = min(rows, 256)
     parts = rows // part
     factor = math.log2(math.e) * head_width ** (-0.5)
-    for place in range(TOPN):
-        here = slice(place * block_len, (place + 1) * block_len)
-        number = number_at(place)
-        slot = slot_at(number)
-        is_own = (number == tile_number).astype(jnp.int32)
-        key_part[here, :head_width] = pool[slot, :, :head_width]
-        key_part[here, head_width:] = mask_bank[is_own]
-        value_part[here, :head_width] = pool[slot, :, head_width:]
-
-    def score(i):
+
+    def gather(u):
+        number_at, slot_at, tile_number, _, _ = units[u]
+        for place in range(TOPN):
+            here = slice(place * block_len, (place + 1) * block_len)
+            number = number_at(place)
+            slot = slot_at(number)
+            is_own = (number == tile_number).astype(jnp.int32)
+            key_parts[u, here, :head_width] = pool[slot, :, :head_width]
+            key_parts[u, here, head_width:] = mask_bank[is_own]
+            value_parts[u, here, :head_width] = pool[slot, :, head_width:]
+
+    def score(u, i):
         here = pl.ds(i * part, part)
-        query = jnp.concatenate([query_at(here), token_hot[here]], axis=1)
-        scores_part[i % 2] = lax.dot_general(
-            query, key_part[...], (((1,), (1,)), ((), ())), preferred_element_type=jnp.float32
+        query = jnp.concatenate([units[u][3](here), token_hot[here]], axis=1)
+        scores_parts[u, i % 2] = lax.dot_general(
+            query, key_parts[u], (((1,), (1,)), ((), ())), preferred_element_type=jnp.float32
         )
 
-    score(0)
-    for i in range(parts):
-        if i + 1 < parts:
-            score(i + 1)
-        scores = scores_part[i % 2]
+    def mix(u, i):
+        scores = scores_parts[u, i % 2]
         top = jnp.max(scores, axis=-1, keepdims=True)
         weights = jnp.exp2((scores - top) * factor).astype(jnp.bfloat16)
-        mixed = jnp.dot(weights, value_part[...], preferred_element_type=jnp.float32)
-        store(i * part, part, mixed[:, :head_width] / mixed[:, head_width:])
+        mixed = jnp.dot(weights, value_parts[u], preferred_element_type=jnp.float32)
+        units[u][4](i * part, part, mixed[:, :head_width] / mixed[:, head_width:])
+
+    steps = [(u, i) for u in range(len(units)) for i in range(parts)]
+    gather(0)
+    score(0, 0)
+    for n, (u, i) in enumerate(steps):
+        if n + 1 < len(steps):
+            ahead = steps[n + 1]
+            if i == 0 and u + 1 < len(units):
+                gather(u + 1)
+            score(*ahead)
+        mix(u, i)
 
 
 def finish(
@@ -75,42 +88,47 @@
     out_ref,
     block_scores_ref,
     wide,
-    key_part,
-    value_part,
-    scores_part,
+    key_parts,
+    value_parts,
+    scores_parts,
     token_hot,
     mask_bank,
 ):
     _, groups, blk_dev, heads_local, block_len, head_width = shape
     rows = block_len * heads_local
     rank = lax.axis_index("seq")
-    t = pl.program_id(0)
+    step = pl.program_id(0)
     last = groups - 1
-
-    @pl.when(t == 0)
+    width = wide.shape[0]
+
+    @pl.when(step == 0)
     def _():
-        prepare(shape, token_hot, mask_bank, value_part)
+        prepare(shape, token_hot, mask_bank, value_parts)
         lines = pooled_ref.shape[0]
         line_tile = lax.broadcasted_iota(jnp.int32, (lines, 1), 0) // (lines // blk_dev)
         scale = (rank * blk_dev + line_tile + 1).astype(jnp.float32) / (block_len * HPG)
         block_scores_ref[...] = pooled_ref[...] * scale
 
-    wide[...] = partial_ref[0].astype(jnp.float32).reshape(rows * groups, head_width)
-
-    def store(start, count, result):
-        wide[pl.ds(start * groups + last, count, stride=groups)] = result
-
-    attend_unit(
-        shape,
-        pool_ref,
-        lambda place: pick_ref[t, last, place],
-        lambda number: slot_ref[last, number],
-        rank * blk_dev + t,
-        lambda here: query_ref[0, here],
-        store,
-        (key_part, value_part, scores_part, token_hot, mask_bank),
-    )
-    out_ref[0] = wide[...].reshape(rows, groups, head_width).astype(jnp.bfloat16)
+    def unit(u):
+        t = step * width + u
+
+        def store(start, count, result):
+            wide[u, pl.ds(start * groups + last, count, stride=groups)] = result
+
+        return (
+            lambda place: pick_ref[t, last, place],
+            lambda number: slot_ref[last, number],
+            rank * blk_dev + t,
+            lambda here: query_ref[u, here],
+            store,
+        )
+
+    for u in range(width):
+        wide[u] = partial_ref[u].astype(jnp.float32).reshape(rows * groups, head_width)
+    work = (key_parts, value_parts, scores_parts, token_hot, mask_bank)
+    attend_units(shape, pool_ref, [unit(u) for u in range(width)], work)
+    for u in range(width):
+        out_ref[u] = wide[u].reshape(rows, groups, head_width).astype(jnp.bfloat16)
 
 
 def mega(
@@ -135,10 +153,9 @@
     queries,
     wide_out,
     stage,
-    rows_stage,
-    key_part,
-    value_part,
-    scores_part,
+    key_parts,
+    value_parts,
+    scores_parts,
     token_hot,
     mask_bank,
     slot_map,
@@ -160,7 +177,9 @@
 ):
     levels, groups, blk_dev, heads_local, block_len, head_width = shape
     rows = block_len * heads_local
+    tokens = blk_dev * block_len
     per_level = COLS * CORES
+    nblk = levels * per_level * blk_dev
     slots_col = levels * CORES * blk_dev
     picks = CORES * CAP
     f32, bf16 = jnp.float32, jnp.bfloat16
@@ -226,15 +245,47 @@
 
     wanted_copy = remote(wanted, peer_wanted, misc_sem.at[0], misc_sem.at[1], peer)
     slots_copy = pltpu.make_async_copy(slot_map, slot_map_s, misc_sem.at[2])
-    loads = [
-        pltpu.make_async_copy(key_ref, rows_stage.at[0], misc_sem.at[4]),
-        pltpu.make_async_copy(value_ref, rows_stage.at[1], misc_sem.at[5]),
-    ]
-    for load in loads:
-        load.start()
+    def load(slab, kind, ref):
+        return pltpu.make_async_copy(
+            ref.at[slab * rows : (slab + 1) * rows], stage.at[kind], misc_sem.at[4 + kind]
+        )
+
+    load(0, 0, key_ref).start()
+    load(0, 1, value_ref).start()
+
+    own_summary = jnp.swapaxes(summary_ref[...].astype(f32), 0, 1)
+    own_summary = own_summary.reshape(groups * blk_dev, head_width).astype(bf16)
+    summaries[level, col, core] = own_summary
+    for slab in range(tokens // rows):
+        for kind, ref in enumerate((key_ref, value_ref)):
+            load(slab, kind, ref).wait()
+
+            def split(r, slab=slab, kind=kind):
+                source = pl.ds(pl.multiple_of(r * block_len, block_len), block_len)
+                place = pl.multiple_of(slab * rows + r * block_len, block_len)
+                apart = jnp.swapaxes(stage[kind, source].astype(f32), 0, 1).astype(bf16)
+                lanes = slice(kind * head_width, (kind + 1) * head_width)
+                for g in range(groups):
+                    column[level, core, g, pl.ds(place, block_len), lanes] = apart[g]
+
+            loop(heads_local, split)
+            if (slab + 1) * rows < tokens:
+                load(slab + 1, kind, ref).start()
     query_copy(0).start()
-
-    nblk = levels * per_level * blk_dev
+    pl.semaphore_wait(barrier, levels + 1)
+
+    loop(levels, lambda l: keys_up(l, level).start(), level + 1)
+    keys_aside(level, core).start()
+
+    def send_own(g):
+        @pl.when(has_above)
+        def _():
+            up(level, g).start()
+
+    lead = jnp.where(level == 0, groups, jnp.where(level == levels - 2, min(3, groups), 1))
+    loop(lead, send_own)
+    loop(groups, lambda g: aside(level, g, core).start())
+
     number = lax.broadcasted_iota(jnp.int32, (groups, nblk), 1)
     named = jnp.zeros((groups, nblk), jnp.int32)
     for t in range(blk_dev):
@@ -260,36 +311,26 @@
     in_column = lax.rem(device // CORES, COLS) == col
     slot_map[...] = jnp.where(in_column, pair * blk_dev + inside, slots_col + pair * CAP + order)
 
-    own_summary = jnp.swapaxes(summary_ref[...].astype(f32), 0, 1)
-    own_summary = own_summary.reshape(groups * blk_dev, head_width).astype(bf16)
-    summaries[level, col, core] = own_summary
-    prepare(shape, token_hot, mask_bank, value_part)
+    prepare(shape, token_hot, mask_bank, value_parts)
     summaries_wide[...] = jnp.zeros_like(summaries_wide)
-    for kind in range(2):
-        loads[kind].wait()
-
-        def split(r, kind=kind):
-            here = pl.ds(pl.multiple_of(r * block_len, block_len), block_len)
-            apart = jnp.swapaxes(rows_stage[kind, here].astype(f32), 0, 1).astype(bf16)
-            for g in range(groups):
-                column[level, core, g, here, kind * head_width : (kind + 1) * head_width] = apart[g]
-
-        loop(blk_dev, split)
+    wanted_copy.start()
     slots_copy.start()
-    pl.semaphore_wait(barrier, levels + 1)
-
-    loop(levels, lambda l: keys_up(l, level).start(), level + 1)
-    keys_aside(level, core).start()
-    wanted_copy.start()
-
-    def send_own(g):
+
+    def relay(g, l):
+        up(l, g).wait_recv()
+
         @pl.when(has_above)
         def _():
-            up(level, g).start()
-
-    lead = jnp.where(level == 0, groups, jnp.where(level == levels - 2, min(3, groups), 1))
-    loop(lead, send_own)
-    loop(groups, lambda g: aside(level, g, core).start())
+            up(l, g).start()
+
+        aside(l, g, core).start()
+
+    def early(g):
+        relay(g, level - 1)
+
+        @pl.when((level == 1) & (g + 1 >= lead) & (g + 1 < groups))
+        def _():
+            send_own(g + 1)
 
     def spread(t):
         query_copy(t).wait()
@@ -310,6 +351,10 @@
     ]
     for copy in handed_on:
         copy.start()
+
+    @pl.when(level > 0)
+    def _():
+        early(0)
 
     def relay_keys(l):
         keys_up(l, l).wait_recv()
@@ -333,15 +378,6 @@
     local_wanted.wait()
     slots_copy.wait()
     loop(level + 1, widen_keys)
-
-    def relay(g, l):
-        up(l, g).wait_recv()
-
-        @pl.when(has_above)
-        def _():
-            up(l, g).start()
-
-        aside(l, g, core).start()
 
     def take(g, l):
         half = lax.rem(g, 2)
@@ -397,22 +433,27 @@
 
         loop(groups_end, body, first_group)
 
-    def attend(g, t):
+    width = key_parts.shape[0]
+
+    def attend(g, turn):
         half = lax.rem(g, 2)
 
-        def store(start, count, result):
-            wide_out[t, pl.ds(start * groups + g, count, stride=groups)] = result
-
-        attend_unit(
-            shape,
-            cur.at[half],
-            lambda place: pick_ref[t, g, place],
-            lambda number: slot_map_s[g, number],
-            rank * blk_dev + t,
-            lambda here: queries[g, t, here],
-            store,
-            (key_part, value_part, scores_part, token_hot, mask_bank),
-        )
+        def unit(u):
+            t = turn * width + u
+
+            def store(start, count, result):
+                wide_out[t, pl.ds(start * groups + g, count, stride=groups)] = result
+
+            return (
+                lambda place: pick_ref[t, g, place],
+                lambda number: slot_map_s[g, number],
+                rank * blk_dev + t,
+                lambda here: queries[g, t, here],
+                store,
+            )
+
+        work = (key_parts, value_parts, scores_parts, token_hot, mask_bank)
+        attend_units(shape, cur.at[half], [unit(u) for u in range(width)], work)
 
     def put_out(t):
         @pl.when(t > 1)
@@ -427,17 +468,24 @@
         here = pl.ds(kind * slots_col + l * count, count)
         return pltpu.make_async_copy(cur.at[(groups - 1) % 2, here], pool_out.at[here], pool_sem.at[kind, l])
 
-    relay_at = [0] + [(i - 1) * (blk_dev - 2) // max(levels - 2, 1) for i in range(1, levels)]
-    take_at = [0] + [min(spot + 1, blk_dev) for spot in relay_at[1:]]
+    turns = blk_dev // width
+    relay_at = [0] + [(i - 1) * (turns - 1) // max(levels - 2, 1) for i in range(1, levels)]
+    take_at = [0] + [min(spot + 1, turns) for spot in relay_at[1:]]
 
     def relays(g, t, i):
-        @pl.when((t == relay_at[i]) & (level >= i))
+        due = (t == relay_at[i]) & (level >= i)
+        if i == 1:
+            due = due & (g > 0) & (level == levels - 1)
+
+        @pl.when(due)
         def _():
             relay(g, level - i)
 
-        @pl.when((t == relay_at[i]) & (level == i) & (g + 1 >= lead) & (g + 1 < groups))
-        def _():
-            send_own(g + 1)
+        if i > 1:
+
+            @pl.when((t == relay_at[i]) & (level == i) & (g + 1 >= lead) & (g + 1 < groups))
+            def _():
+                send_own(g + 1)
 
     def takes(g, t, i):
         @pl.when((t == take_at[i]) & (level >= i))
@@ -445,30 +493,36 @@
             take(g, level - i)
 
     def main(g):
-        def tile(t):
+        def tiles(turn):
             for i in range(levels):
-                if i > 0 and relay_at[i] < blk_dev:
-                    relays(g, t, i)
-                if take_at[i] < blk_dev:
-                    takes(g, t, i)
+                if i > 0 and relay_at[i] < turns:
+                    relays(g, turn, i)
+                if take_at[i] < turns:
+                    takes(g, turn, i)
 
             @pl.when(g > 0)
             def _():
-                attend(g - 1, t)
+                attend(g - 1, turn)
 
             @pl.when(g == groups - 1)
             def _():
-                put_out(t)
-
-        loop(blk_dev, tile)
+                for u in range(width):
+                    put_out(turn * width + u)
+
+        loop(turns, tiles)
         for i in range(1, levels):
-            if relay_at[i] == blk_dev:
-                relays(g, blk_dev, i)
+            if relay_at[i] == turns:
+                relays(g, turns, i)
+
+        @pl.when(has_above & (level > 0) & (g + 1 < groups))
+        def _():
+            early(g + 1)
+
         first_tile, end_tile = g * blk_dev // groups, (g + 1) * blk_dev // groups
         loop(end_tile, lambda t: score_tile(t, 0, groups // 2), first_tile)
         for i in range(1, levels):
-            if take_at[i] == blk_dev:
-                takes(g, blk_dev, i)
+            if take_at[i] == turns:
+                takes(g, turns, i)
         loop(end_tile, lambda t: score_tile(t, groups // 2, groups), first_tile)
         take_peer(g)
 
@@ -518,6 +572,7 @@
     wide = 2 * head_width
     served = CORES * CAP * block_len
     part = min(rows, 256)
+    width = 2 - blk_dev % 2
     dma = pltpu.SemaphoreType.DMA
     smem = pl.BlockSpec(memory_space=pltpu.SMEM)
     vmem = pl.BlockSpec(memory_space=pltpu.VMEM)
@@ -545,10 +600,9 @@
             pltpu.VMEM((groups, blk_dev, rows, head_width), bf16),
             pltpu.VMEM((blk_dev, rows * groups, head_width), f32),
             pltpu.VMEM((2, rows, groups, head_width), bf16),
-            pltpu.VMEM((2, tok_rows, groups, head_width), bf16),
-            pltpu.VMEM((TOPN * block_len, wide), bf16),
-            pltpu.VMEM((TOPN * block_len, wide), bf16),
-            pltpu.VMEM((2, part, TOPN * block_len), f32),
+            pltpu.VMEM((width, TOPN * block_len, wide), bf16),
+            pltpu.VMEM((width, TOPN * block_len, wide), bf16),
+            pltpu.VMEM((width, 2, part, TOPN * block_len), f32),
             pltpu.VMEM((rows, head_width), bf16),
             pltpu.VMEM((2, block_len, head_width), bf16),
             pltpu.VMEM((groups, nblk), jnp.int32),
@@ -569,21 +623,21 @@
     groups_out = shared.shape[2]
     whole = pl.BlockSpec((slots, block_len, wide), lambda t: (0, 0, 0))
     lines = pl.BlockSpec((blk_dev * groups_out, nblk), lambda t: (0, 0))
-    tile = pl.BlockSpec((1, rows, groups, head_width), lambda t: (t, 0, 0, 0))
+    tile = pl.BlockSpec((width, rows, groups, head_width), lambda t: (t, 0, 0, 0))
     attended, block_scores = pl.pallas_call(
         functools.partial(finish, shape),
-        grid=(blk_dev,),
-        in_specs=[smem, smem, tile, pl.BlockSpec((1, rows, head_width), lambda t: (t, 0, 0)), whole, lines],
+        grid=(blk_dev // width,),
+        in_specs=[smem, smem, tile, pl.BlockSpec((width, rows, head_width), lambda t: (t, 0, 0)), whole, lines],
         out_specs=[tile, lines],
         out_shape=[
             jax.ShapeDtypeStruct((blk_dev, rows, groups, head_width), bf16),
             jax.ShapeDtypeStruct((blk_dev * groups_out, nblk), f32),
         ],
         scratch_shapes=[
-            pltpu.VMEM((rows * groups, head_width), f32),
-            pltpu.VMEM((TOPN * block_len, wide), bf16),
-            pltpu.VMEM((TOPN * block_len, wide), bf16),
-            pltpu.VMEM((2, part, TOPN * block_len), f32),
+            pltpu.VMEM((width, rows * groups, head_width), f32),
+            pltpu.VMEM((width, TOPN * block_len, wide), bf16),
+            pltpu.VMEM((width, TOPN * block_len, wide), bf16),
+            pltpu.VMEM((width, 2, part, TOPN * block_len), f32),
             pltpu.VMEM((rows, head_width), bf16),
             pltpu.VMEM((2, block_len, head_width), bf16),
         ],

time: 170 us -> 167 us (0.982)
  Pallas kernels: 168 us -> 165 us
    pallas_call x1, Pallas kernels: 14.5 us -> 12.5 us  [local(): pl.pallas_call(functools.partial(finish, shape), grid=(blk_dev // width,)...]
where the time goes in v4:
time: 167 us; the launch traced here: 166 us
  Pallas kernels  165 us (99%)
    pallas_call x1, Pallas kernels, local(): pl.pallas_call(functools.partial(mega, shape), in_specs=[smem, vmem, vmem...  153 us
    pallas_call x1, Pallas kernels, local(): pl.pallas_call(functools.partial(finish, shape), grid=(blk_dev // width,)...  12.5 us

profile of v4, /device:TPU:24, one launch (start us, length us, event | category | flops | bytes accessed | tf_op | source)
XLA Modules:
  0.0 165.9 jit_solution(14712651545822526625)
XLA Ops:
  0.6 152.8 %shard_map.68 = (bf16[8,512,8,128]{3,2,1,0:T(8,128)(2,1)}, f32[64,128]{1,0:T(8,128)}, bf16[80,64,256]{2,1,0:T(8,128)(2,1)}, bf16[8,512,128]{2,1,0:T(8,128)(2,1)}, s32[8,128]{1,0:T(8,128)}) custom-call(s32[8,8,16]{2,1,0:T(8,128)} %bitcast.10, s32[8,8,16]{2,1,0:T(8,128)} %bitcast.11, bf16[8,8,128]{2,1,0:T(8,128)(2,1)} %bitcast.13, ...), custom_call_target="tpu_custom_call" | custom-call | tf_op jit(solution)/shard_map/pallas_call | solution.py:582
  153.4 12.5 %shard_map.69 = (bf16[8,512,8,128]{3,2,1,0:T(8,128)(2,1)}, f32[64,128]{1,0:T(8,128)}) custom-call(s32[8,8,16]{2,1,0:T(8,128)} %bitcast.12, s32[8,128]{1,0:T(8,128)} %get-tuple-element.9.slot_ref, bf16[8,512,8,128]{3,2,1,0:T(8,128)(2,1)} %get-tuple-element.10.partial_ref, bf16[8,512,128]{2,1,0:T(8,128)(2,1)} %get-tuple-element.11.query_ref, ...), custom_call_target="tpu_custom_call" | custom-call | tf_op jit(solution)/shard_map/pallas_call | solution.py:627

commit v5 on v4

--- a/solution.py
+++ b/solution.py
@@ -519,11 +519,10 @@
             early(g + 1)
 
         first_tile, end_tile = g * blk_dev // groups, (g + 1) * blk_dev // groups
-        loop(end_tile, lambda t: score_tile(t, 0, groups // 2), first_tile)
         for i in range(1, levels):
             if take_at[i] == turns:
                 takes(g, turns, i)
-        loop(end_tile, lambda t: score_tile(t, groups // 2, groups), first_tile)
+        loop(end_tile, lambda t: score_tile(t, 0, groups), first_tile)
         take_peer(g)
 
     loop(groups, main)

time: 167 us -> 165 us (0.988)
  no operation moved by 1% of the time
where the time goes in v5:
time: 165 us; the launch traced here: 164 us
  Pallas kernels  164 us (99%)
    pallas_call x1, Pallas kernels, local(): pl.pallas_call(functools.partial(mega, shape), in_specs=[smem, vmem, vmem...  151 us
    pallas_call x1, Pallas kernels, local(): pl.pallas_call(functools.partial(finish, shape), grid=(blk_dev // width,)...  12.5 us

profile of v5, /device:TPU:24, one launch (start us, length us, event | category | flops | bytes accessed | tf_op | source)
XLA Modules:
  0.0 164.3 jit_solution(16409452791131677302)
XLA Ops:
  0.6 151.1 %shard_map.68 = (bf16[8,512,8,128]{3,2,1,0:T(8,128)(2,1)}, f32[64,128]{1,0:T(8,128)}, bf16[80,64,256]{2,1,0:T(8,128)(2,1)}, bf16[8,512,128]{2,1,0:T(8,128)(2,1)}, s32[8,128]{1,0:T(8,128)}) custom-call(s32[8,8,16]{2,1,0:T(8,128)} %bitcast.10, s32[8,8,16]{2,1,0:T(8,128)} %bitcast.11, bf16[8,8,128]{2,1,0:T(8,128)(2,1)} %bitcast.13, ...), custom_call_target="tpu_custom_call" | custom-call | tf_op jit(solution)/shard_map/pallas_call | solution.py:581
  151.8 12.5 %shard_map.69 = (bf16[8,512,8,128]{3,2,1,0:T(8,128)(2,1)}, f32[64,128]{1,0:T(8,128)}) custom-call(s32[8,8,16]{2,1,0:T(8,128)} %bitcast.12, s32[8,128]{1,0:T(8,128)} %get-tuple-element.9.slot_ref, bf16[8,512,8,128]{3,2,1,0:T(8,128)(2,1)} %get-tuple-element.10.partial_ref, bf16[8,512,128]{2,1,0:T(8,128)(2,1)} %get-tuple-element.11.query_ref, ...), custom_call_target="tpu_custom_call" | custom-call | tf_op jit(solution)/shard_map/pallas_call | solution.py:626
